TPU v7x, 128 devices: a whole 4x4x4 slice. The times are simulated.
128 devices in a mesh: gx: 16 (over y, z), gy: 8 (over x, core).
Axes of the slice: x: 4, y: 4, z: 4, core: 2. Of those that a mesh axis runs over, the one named last changes fastest.
Arguments:
- velocity: float32 [3, 128, 512, 384], P(None, 'gx', 'gy')
- target_profile: float32 [2, 384], replicated, may hold values from 0.5 to 1.5
- disc_turbine: int32 [128, 4], P(('gx', 'gy')), may hold values from -1 to 99, as said below
- disc_start: int32 [3, 128, 4], P(None, ('gx', 'gy')), may hold values from 0 to 256, as said below
- disc_weight: float32 [128, 4, 16, 128], P(('gx', 'gy')), may hold values from 0.2 to 1
- turbine_owner: int32 [100], replicated, may hold values from 0 to 127, as said below
- mode_flag: int32 [100], replicated, may hold values from 0 to 2
- controller_state: float32 [128, 4], P(('gx', 'gy')), may hold values from -4 to 4
Outputs:
- advanced_velocity: float32 [3, 128, 512, 384], P(None, 'gx', 'gy')
- profiles: float32 [4, 384], replicated
- thrust_setpoint: float32 [100], replicated
- controller_next: float32 [128, 4], P(('gx', 'gy'))
Inputs may be any that keep to these rules, and one draw needn't show every extreme that they name: `disc_turbine`: -1 marks an empty slot; every turbine number appears in at least one slot; some device has all 4 slots filled. `disc_start`: row 0 is a cell of the device's block along the first dimension, 0 to 7; row 1 the first of 16 cells along the second, 0 to 48; row 2 the first of 128 heights, 0 to 256. `turbine_owner`: no device owns more than 4 turbines, and some device owns exactly 4.
All inputs are finite; a program needn't handle non-finite values.
Results may differ from a plain program's by a relative error of at most 0.00013.
Values sent between devices are 32-bit elements; how exact they have to be, the bound alone decides.
No kernel may reach another device: no remote copies, remote signals or barrier semaphores. Data moves between devices by JAX's collectives and lax.ppermute only.
A program may use at most 128 MiB of HBM per device.

v0:
```python
import jax
import jax.numpy as jnp
from jax import lax
from jax.sharding import Mesh
from jax.sharding import PartitionSpec as P

STEPS = 4
GX = ("gx_0", "gx_1")
GY = ("gy_0", "gy_1")
GX_GY = ("gx_0", "gx_1", "gy_0", "gy_1")


VISCOSITY = 0.1
TIME_STEP = 0.2
RELAX_TIME = 2.0
CONTROL_STEP = 0.5
GAIN_PROPORTIONAL = 2.0
GAIN_INTEGRAL = 1.0
HIGHEST = lax.Precision.HIGHEST


def by_axis(shard, axes):
    for axis in axes:
        shard = lax.psum(shard, axis)
    return shard


def padded_2(shard, sides, width):
    edges = {}
    for axis, dim in sides:
        size, length = (lax.axis_size(axis), shard.shape[dim])
        up = [(i, (i + 1) % size) for i in range(size)]
        last = lax.slice_in_dim(shard, length - width, length, axis=dim)
        first = lax.slice_in_dim(shard, 0, width, axis=dim)
        edges[dim] = (
            lax.ppermute(last, axis, up),
            lax.ppermute(first, axis, [(b, a) for a, b in up]),
        )
    done = []
    for _, dim in sides:
        low, high = edges[dim]
        around = [(width, width) if d in done else (0, 0) for d in range(shard.ndim)]
        shard = jnp.concatenate([jnp.pad(low, around), shard, jnp.pad(high, around)], axis=dim)
        done.append(dim)
    return shard


def pad_height(block):
    return jnp.pad(block, ((0, 0), (0, 0), (0, 0), (2, 2)))


def tendency(block):
    length_x = block.shape[1] - 4
    length_y = block.shape[2] - 4
    length_z = block.shape[3] - 4

    def shifted(offset_x, offset_y, offset_z):
        return block[
            :,
            2 + offset_x : 2 + offset_x + length_x,
            2 + offset_y : 2 + offset_y + length_y,
            2 + offset_z : 2 + offset_z + length_z,
        ]

    centre = shifted(0, 0, 0)
    grad_x = (
        8.0 * (shifted(1, 0, 0) - shifted(-1, 0, 0)) - (shifted(2, 0, 0) - shifted(-2, 0, 0))
    ) / 12.0
    grad_y = (
        8.0 * (shifted(0, 1, 0) - shifted(0, -1, 0)) - (shifted(0, 2, 0) - shifted(0, -2, 0))
    ) / 12.0
    grad_z = (
        8.0 * (shifted(0, 0, 1) - shifted(0, 0, -1)) - (shifted(0, 0, 2) - shifted(0, 0, -2))
    ) / 12.0
    laplacian = (
        shifted(1, 0, 0)
        + shifted(-1, 0, 0)
        + (shifted(0, 1, 0) + shifted(0, -1, 0))
        + (shifted(0, 0, 1) + shifted(0, 0, -1))
        - 6.0 * centre
    )
    advection = centre[0:1] * grad_x + centre[1:2] * grad_y + centre[2:3] * grad_z
    return VISCOSITY * laplacian - advection


def control_terms(mode_flag):
    rated_speed = jnp.where(mode_flag == 0, 0.7, jnp.where(mode_flag == 1, 0.9, 1.1)).astype(
        jnp.float32
    )
    bias_terms = jnp.where(mode_flag == 0, 1.0, jnp.where(mode_flag == 1, 0.0, -1.0)).astype(
        jnp.float32
    )
    return (rated_speed, bias_terms)


def owner_rank(turbine_owner):
    turbines = turbine_owner.shape[0]
    same_owner = turbine_owner[:, None] == turbine_owner[None, :]
    earlier = (
        jnp.arange(turbines, dtype=jnp.int32)[None, :]
        < jnp.arange(turbines, dtype=jnp.int32)[:, None]
    )
    return jnp.sum((same_owner & earlier).astype(jnp.int32), axis=1)


def thrust_from(bias_terms, speed_error, integral):
    return 0.1 + 0.9 * jax.nn.sigmoid(
        bias_terms - GAIN_PROPORTIONAL * speed_error - GAIN_INTEGRAL * integral
    )


def local(
    velocity,
    target_profile,
    disc_turbine,
    disc_start,
    disc_weight,
    turbine_owner,
    mode_flag,
    controller_state,
):
    blocks_x = lax.axis_size(GX)
    blocks_y = lax.axis_size(GY)
    devices = blocks_x * blocks_y
    device_me = lax.axis_index(GX) * blocks_y + lax.axis_index(GY)
    length_x = velocity.shape[1]
    length_y = velocity.shape[2]
    length_z = velocity.shape[3]
    turbines = mode_flag.shape[0]
    owned = controller_state.shape[1]
    slots = disc_turbine.shape[1]
    tile_y = disc_weight.shape[2]
    tile_z = disc_weight.shape[3]
    weights_local = disc_weight[0]
    start_x = disc_start[0, 0]
    start_y = disc_start[1, 0]
    start_z = disc_start[2, 0]
    turbine_ids = jnp.arange(turbines, dtype=jnp.int32)
    slot_onehot = (disc_turbine[0][:, None] == turbine_ids[None, :]).astype(jnp.float32)
    area_part = jnp.dot(jnp.sum(weights_local, axis=(1, 2)), slot_onehot, precision=HIGHEST)
    disc_area = by_axis(area_part, GX_GY)
    owner_slot = owner_rank(turbine_owner)
    owner_column = turbine_owner * owned + owner_slot
    pick_table = (
        owner_column[:, None] == jnp.arange(devices * owned, dtype=jnp.int32)[None, :]
    ).astype(jnp.float32)
    mine_table = (
        (turbine_owner[:, None] == device_me)
        & (owner_slot[:, None] == jnp.arange(owned, dtype=jnp.int32)[None, :])
    ).astype(jnp.float32)
    live_slot = jnp.sum(mine_table, axis=0)
    rated_speed, bias_terms = control_terms(mode_flag)
    integral = controller_state[0]
    state_all = lax.all_gather(controller_state[0], GX_GY, axis=0, tiled=True)
    integral_all = jnp.dot(pick_table, state_all, precision=HIGHEST)
    plane_cells = float(length_x * blocks_x * length_y * blocks_y)
    profiles = jnp.zeros((4, length_z), jnp.float32)
    thrust = jnp.zeros((turbines,), jnp.float32)
    for turn_index in range(STEPS):
        streamwise = velocity[0]
        contribution = jnp.stack(
            [
                jnp.sum(
                    weights_local[slot_index]
                    * lax.dynamic_slice(
                        streamwise,
                        (start_x[slot_index], start_y[slot_index], start_z[slot_index]),
                        (1, tile_y, tile_z),
                    )[0]
                )
                for slot_index in range(slots)
            ]
        )
        numerator_part = jnp.dot(contribution, slot_onehot, precision=HIGHEST)
        plane_part = jnp.stack(
            [
                jnp.sum(velocity[0], axis=(0, 1)),
                jnp.sum(velocity[1], axis=(0, 1)),
                jnp.sum(velocity[2], axis=(0, 1)),
                jnp.sum(velocity[0] * velocity[2], axis=(0, 1)),
            ]
        )
        plane_sums, numerator = (by_axis(plane_part, GX_GY), by_axis(numerator_part, GX_GY))
        disc_speed = numerator / disc_area
        speed_error = disc_speed - rated_speed
        integral_all = integral_all + CONTROL_STEP * speed_error
        thrust = thrust_from(bias_terms, speed_error, integral_all)
        thrust_factor = 0.5 * thrust * disc_speed * jnp.abs(disc_speed)
        slot_factor = jnp.dot(slot_onehot, thrust_factor, precision=HIGHEST)
        force_field = jnp.zeros((length_x, length_y, length_z), jnp.float32)
        for slot_index in range(slots):
            corner = (start_x[slot_index], start_y[slot_index], start_z[slot_index])
            previous = lax.dynamic_slice(force_field, corner, (1, tile_y, tile_z))
            force_field = lax.dynamic_update_slice(
                force_field,
                previous - slot_factor[slot_index] * weights_local[slot_index][None],
                corner,
            )
        plane_means = plane_sums / plane_cells
        profiles = profiles + jnp.stack(
            [
                plane_means[0],
                plane_means[1],
                plane_means[2],
                plane_means[3] - plane_means[0] * plane_means[2],
            ]
        )
        nudging = (target_profile - plane_means[0:2]) / RELAX_TIME
        padded = padded_2(velocity, ((GX, 1), (GY, 2)), 2)
        changes = tendency(pad_height(padded))
        velocity = jnp.stack(
            [
                velocity[0] + TIME_STEP * (changes[0] + nudging[0][None, None, :] + force_field),
                velocity[1] + TIME_STEP * (changes[1] + nudging[1][None, None, :]),
                velocity[2] + TIME_STEP * changes[2],
            ]
        )
    integral = jnp.dot(integral_all, mine_table, precision=HIGHEST) + (1.0 - live_slot) * integral
    return (velocity, profiles / STEPS, thrust, integral[None, :])


def solution(mesh):
    torus = Mesh(mesh.devices.reshape(4, 4, 4, 2), ("gx_0", "gx_1", "gy_0", "gy_1"))
    placed = (
        P(None, GX, GY, None),
        P(),
        P(GX_GY, None),
        P(None, GX_GY, None),
        P(GX_GY, None, None, None),
        P(),
        P(),
        P(GX_GY, None),
    )
    return jax.shard_map(
        local,
        mesh=torus,
        in_specs=placed,
        out_specs=(P(None, GX, GY, None), P(), P(), P(GX_GY, None)),
        check_vma=False,
    )
```

profile of v0, /device:TPU:1, one launch (start us, length us, event | category | flops | bytes accessed | tf_op | source)
XLA Modules:
  0.0 434.8 jit_solution(4336565369596881345)
XLA Ops:
  3.3 2.3 fusion.241
  5.6 1.7 collective-permute-start.1
  7.4 4.6 %collective-permute-start = (f32[3,2,64,384]{3,2,1,0:T(8,128)}, f32[3,2,64,384]{3,2,1,0:T(8,128)}, u32[]{:S(2)}, u32[]{:S(2)}) collective-permute-start(f32[3,2,64,384]{3,2,1,0:T(8,128)} %get-tuple-element.144), channel_id=1, source_target_pairs={{8,0},{16,8},{24,16},{32,24},{40,32},{48,40},{56,48},{64,56},{72,6... | collective-permute-start | bytes 1769480 | tf_op jit(solution)/shard_map/ppermute | solution.py:37
  39.7 2.7 convolution_bitcast_fusion.10
  42.4 6.9 %all-reduce.24 = (f32[4,384]{1,0:T(4,128)S(1)}, f32[100]{0:T(128)S(1)}, f32[100]{0:T(128)S(1)}) all-reduce(f32[4,384]{1,0:T(4,128)S(1)} %pad_maximum_fusion.12, f32[100]{0:T(128)S(1)} %convolution_bitcast_fusion.10, f32[100]{0:T(128)S(1)} %convolution_bitcast_fusion.9), channel_id=1, replica_groups=mesh['gx_0'=4,'gx_1'=4,'gy_0'=4,'gy_1'=2] {'gx_0'}, use_global_device_ids=true, to_apply=%region_4.0 | all-reduce | flops 1736 | bytes 13888 | tf_op jit(solution)/shard_map/psum | solution.py:24
  49.3 7.3 %all-reduce.20 = (f32[4,384]{1,0:T(4,128)S(1)}, f32[100]{0:T(128)S(1)}, f32[100]{0:T(128)S(1)}) all-reduce(f32[4,384]{1,0:T(4,128)S(1)} %get-tuple-element.65, f32[100]{0:T(128)S(1)} %get-tuple-element.66, f32[100]{0:T(128)S(1)} %get-tuple-element.67), channel_id=1, replica_groups=mesh['gx_0'=4,'gx_1'=4,'gy_0'=4,'gy_1'=2] {'gx_1'}, use_global_device_ids=true, to_apply=%region_5.0 | all-reduce | flops 1736 | bytes 13888 | tf_op jit(solution)/shard_map/psum | solution.py:24
  56.6 9.7 %all-reduce.16 = (f32[4,384]{1,0:T(4,128)S(1)}, f32[100]{0:T(128)S(1)}, f32[100]{0:T(128)S(1)}) all-reduce(f32[4,384]{1,0:T(4,128)S(1)} %get-tuple-element.56, f32[100]{0:T(128)S(1)} %get-tuple-element.57, f32[100]{0:T(128)S(1)} %get-tuple-element.58), channel_id=1, replica_groups=mesh['gx_0'=4,'gx_1'=4,'gy_0'=4,'gy_1'=2] {'gy_0'}, use_global_device_ids=true, to_apply=%region_6.0 | all-reduce | flops 1736 | bytes 13888 | tf_op jit(solution)/shard_map/psum | solution.py:24
  66.4 6.2 %all-reduce.28 = (f32[4,384]{1,0:T(4,128)S(1)}, f32[100]{0:T(128)S(1)}, f32[100]{0:T(128)S(1)}) all-reduce(f32[4,384]{1,0:T(4,128)S(1)} %get-tuple-element.47, f32[100]{0:T(128)S(1)} %get-tuple-element.48, f32[100]{0:T(128)S(1)} %get-tuple-element.49), channel_id=1, replica_groups=mesh['gx_0'=4,'gx_1'=4,'gy_0'=4,'gy_1'=2] {'gy_1'}, use_global_device_ids=true, to_apply=%region_7.8 | all-reduce | flops 1736 | bytes 13888 | tf_op jit(solution)/shard_map/psum | solution.py:24
  73.3 63.1 %all-reduce.12 = f32[512]{0:T(512)S(1)} all-reduce(f32[512]{0:T(512)S(1)} %bitcast_dynamic-update-slice_fusion), channel_id=2, replica_groups=mesh['gx_0'=4,'gx_1'=4,'gy_0'=4,'gy_1'=2] {'gx_0','gx_1','gy_0','gy_1'}, use_global_device_ids=true, to_apply=%add.12 | all-reduce | flops 512 | bytes 4096 | tf_op jit(solution)/shard_map/all_gather | solution.py:154
  147.5 1.6 constant_dynamic-update-slice_fusion
  149.2 2.7 select_maximum_fusion.18
  151.9 8.2 %fusion.33 = f32[3,8,64,384]{3,2,1,0:T(8,128)S(1)} fusion(f32[3,12,68,388]{3,2,1,0:T(8,128)S(1)} %select_maximum_fusion.18, f32[3,12,64,384]{3,2,1,0:T(8,128)} %copy-done.15, f32[3,12,2,384]{3,2,1,0:T(2,128)} %copy-done.31, f32[3,12,2,384]{3,2,1,0:T(2,128)} %copy-done.30, f32[3,10,64,384]{3,2,1,0:T(8,128)} %copy-done.16, ...), kind=kLoop, calls=%fused_computation.81 | loop fusion | flops 17694720 | bytes 29712384 | tf_op jit(solution)/shard_map/sub | solution.py:83
  165.7 2.7 convolution_bitcast_fusion.6
  168.3 7.0 %all-reduce.23 = (f32[4,384]{1,0:T(4,128)S(1)}, f32[100]{0:T(128)S(1)}) all-reduce(f32[4,384]{1,0:T(4,128)S(1)} %pad_maximum_fusion.13, f32[100]{0:T(128)S(1)} %convolution_bitcast_fusion.6), channel_id=1, replica_groups=mesh['gx_0'=4,'gx_1'=4,'gy_0'=4,'gy_1'=2] {'gx_0'}, use_global_device_ids=true, to_apply=%region_26.27 | all-reduce | flops 1636 | bytes 13088 | tf_op jit(solution)/shard_map/psum | solution.py:24
  175.3 7.8 %all-reduce.19 = (f32[4,384]{1,0:T(4,128)S(1)}, f32[100]{0:T(128)S(1)}) all-reduce(f32[4,384]{1,0:T(4,128)S(1)} %get-tuple-element.63, f32[100]{0:T(128)S(1)} %get-tuple-element.64), channel_id=1, replica_groups=mesh['gx_0'=4,'gx_1'=4,'gy_0'=4,'gy_1'=2] {'gx_1'}, use_global_device_ids=true, to_apply=%region_27.28 | all-reduce | flops 1636 | bytes 13088 | tf_op jit(solution)/shard_map/psum | solution.py:24
  183.1 6.5 %all-reduce.15 = (f32[4,384]{1,0:T(4,128)S(1)}, f32[100]{0:T(128)S(1)}) all-reduce(f32[4,384]{1,0:T(4,128)S(1)} %get-tuple-element.54, f32[100]{0:T(128)S(1)} %get-tuple-element.55), channel_id=1, replica_groups=mesh['gx_0'=4,'gx_1'=4,'gy_0'=4,'gy_1'=2] {'gy_0'}, use_global_device_ids=true, to_apply=%region_28.29 | all-reduce | flops 1636 | bytes 13088 | tf_op jit(solution)/shard_map/psum | solution.py:24
  189.6 8.4 %all-reduce.27 = (f32[4,384]{1,0:T(4,128)S(1)}, f32[100]{0:T(128)S(1)}) all-reduce(f32[4,384]{1,0:T(4,128)S(1)} %get-tuple-element.45, f32[100]{0:T(128)S(1)} %get-tuple-element.46), channel_id=1, replica_groups=mesh['gx_0'=4,'gx_1'=4,'gy_0'=4,'gy_1'=2] {'gy_1'}, use_global_device_ids=true, to_apply=%region_29.30 | all-reduce | flops 1636 | bytes 13088 | tf_op jit(solution)/shard_map/psum | solution.py:24
  203.9 2.7 dynamic_update_slice.52
  208.0 2.8 dynamic_update_slice.53
  210.7 1.5 bitcast_subtract_fusion.7
  212.2 2.7 dynamic_update_slice.54
  214.9 1.5 bitcast_subtract_fusion.6
  216.4 2.8 dynamic_update_slice.55
  220.5 7.7 %select_maximum_fusion.12 = f32[3,12,68,388]{3,2,1,0:T(8,128)S(1)} fusion(f32[3,12,2,384]{3,2,1,0:T(2,128)S(1)} %pad.41, f32[3,12,2,384]{3,2,1,0:T(2,128)S(1)} %pad.42, f32[3,2,64,384]{3,2,1,0:T(8,128)} %collective-permute-done.4, f32[3,2,64,384]{3,2,1,0:T(8,128)} %collective-permute-done.5, f32[1,8,64,384]{3,2,1,0:T(8,128)S(1)} %copy-done.11, ...), kind=kLoop, calls=%fused_computation.14 | loop fusion | flops 15197184 | bytes 7559424 | tf_op jit(solution)/shard_map/concatenate | solution.py:43
  228.3 5.5 %pad_maximum_fusion = (f32[3,12,66,384]{3,2,1,0:T(8,128)}, f32[3,12,66,384]{3,2,1,0:T(8,128)}) fusion(f32[3,12,2,384]{3,2,1,0:T(2,128)S(1)} %pad.41, f32[3,2,64,384]{3,2,1,0:T(8,128)} %collective-permute-done.4, f32[1,8,64,384]{3,2,1,0:T(8,128)S(1)} %copy-done.11, f32[1,8,64,384]{3,2,1,0:T(8,128)S(1)} %copy-done.9, f32[1,8,64,384]{3,2,1,0:T(8,128)S(1)} %bitcast.371, ...), kind=kLoop, calls=%fused_computation.27 | loop fusion | flops 9123840 | bytes 11059200 | tf_op jit(solution)/shard_map/concatenate | solution.py:43
  233.8 4.0 pad_maximum_fusion.3
  237.8 9.0 %fusion.24 = f32[3,8,64,384]{3,2,1,0:T(8,128)S(1)} fusion(f32[3,12,68,388]{3,2,1,0:T(8,128)S(1)} %select_maximum_fusion.12, f32[3,12,66,384]{3,2,1,0:T(8,128)} %get-tuple-element.108, f32[3,12,66,384]{3,2,1,0:T(8,128)} %get-tuple-element.107, f32[3,10,64,384]{3,2,1,0:T(8,128)} %get-tuple-element.129, f32[3,10,64,384]{3,2,1,0:T(8,128)} %get-tuple-element.128, ...), kind=kLoop, calls=%fused_computation.69 | loop fusion | flops 16515072 | bytes 35389440 | tf_op jit(solution)/shard_map/sub | solution.py:83
  246.9 1.6 multiply_bitcast_fusion.3
  250.2 2.6 fusion.225
  255.1 2.7 convolution_bitcast_fusion.4
  257.8 7.6 %all-reduce.22 = (f32[4,384]{1,0:T(4,128)S(1)}, f32[100]{0:T(128)S(1)}) all-reduce(f32[4,384]{1,0:T(4,128)S(1)} %pad_maximum_fusion.14, f32[100]{0:T(128)S(1)} %convolution_bitcast_fusion.4), channel_id=1, replica_groups=mesh['gx_0'=4,'gx_1'=4,'gy_0'=4,'gy_1'=2] {'gx_0'}, use_global_device_ids=true, to_apply=%region_42.43 | all-reduce | flops 1636 | bytes 13088 | tf_op jit(solution)/shard_map/psum | solution.py:24
  265.4 9.1 %all-reduce.18 = (f32[4,384]{1,0:T(4,128)S(1)}, f32[100]{0:T(128)S(1)}) all-reduce(f32[4,384]{1,0:T(4,128)S(1)} %get-tuple-element.61, f32[100]{0:T(128)S(1)} %get-tuple-element.62), channel_id=1, replica_groups=mesh['gx_0'=4,'gx_1'=4,'gy_0'=4,'gy_1'=2] {'gx_1'}, use_global_device_ids=true, to_apply=%region_43.44 | all-reduce | flops 1636 | bytes 13088 | tf_op jit(solution)/shard_map/psum | solution.py:24
  274.5 8.2 %all-reduce.14 = (f32[4,384]{1,0:T(4,128)S(1)}, f32[100]{0:T(128)S(1)}) all-reduce(f32[4,384]{1,0:T(4,128)S(1)} %get-tuple-element.52, f32[100]{0:T(128)S(1)} %get-tuple-element.53), channel_id=1, replica_groups=mesh['gx_0'=4,'gx_1'=4,'gy_0'=4,'gy_1'=2] {'gy_0'}, use_global_device_ids=true, to_apply=%region_44.45 | all-reduce | flops 1636 | bytes 13088 | tf_op jit(solution)/shard_map/psum | solution.py:24
  282.7 6.8 %all-reduce.26 = (f32[4,384]{1,0:T(4,128)S(1)}, f32[100]{0:T(128)S(1)}) all-reduce(f32[4,384]{1,0:T(4,128)S(1)} %get-tuple-element.43, f32[100]{0:T(128)S(1)} %get-tuple-element.44), channel_id=1, replica_groups=mesh['gx_0'=4,'gx_1'=4,'gy_0'=4,'gy_1'=2] {'gy_1'}, use_global_device_ids=true, to_apply=%region_45.46 | all-reduce | flops 1636 | bytes 13088 | tf_op jit(solution)/shard_map/psum | solution.py:24
  291.3 1.7 collective-permute-start.9
  295.5 2.7 dynamic_update_slice.56
  299.6 2.8 dynamic_update_slice.57
  302.4 1.5 bitcast_subtract_fusion.4
  303.8 2.7 dynamic_update_slice.58
  306.6 1.5 bitcast_subtract_fusion.3
  308.0 2.8 dynamic_update_slice.59
  311.0 7.7 %select_maximum_fusion.6 = f32[3,12,68,388]{3,2,1,0:T(8,128)S(1)} fusion(f32[3,12,2,384]{3,2,1,0:T(2,128)S(1)} %pad.44, f32[3,12,2,384]{3,2,1,0:T(2,128)S(1)} %pad.45, f32[3,2,64,384]{3,2,1,0:T(8,128)S(1)} %collective-permute-done.8, f32[3,2,64,384]{3,2,1,0:T(8,128)} %collective-permute-done.9, f32[1,8,64,384]{3,2,1,0:T(8,128)S(1)} %copy-done.6, ...), kind=kLoop, calls=%fused_computation.8 | loop fusion | flops 15197184 | bytes 7559424 | tf_op jit(solution)/shard_map/concatenate | solution.py:43
  318.7 4.8 %pad_maximum_fusion.1 = (f32[3,12,66,384]{3,2,1,0:T(8,128)}, f32[3,12,66,384]{3,2,1,0:T(8,128)}) fusion(f32[3,12,2,384]{3,2,1,0:T(2,128)S(1)} %pad.44, f32[3,2,64,384]{3,2,1,0:T(8,128)S(1)} %collective-permute-done.8, f32[1,8,64,384]{3,2,1,0:T(8,128)S(1)} %copy-done.6, f32[1,8,64,384]{3,2,1,0:T(8,128)S(1)} %copy-done.4, f32[1,8,64,384]{3,2,1,0:T(8,128)S(1)} %bitcast.366, ...), kind=kLoop, calls=%fused_computation.29 | loop fusion | flops 9123840 | bytes 11059200 | tf_op jit(solution)/shard_map/concatenate | solution.py:43
  323.6 3.0 pad_maximum_fusion.4
  326.5 8.6 %fusion.15 = f32[3,8,64,384]{3,2,1,0:T(8,128)} fusion(f32[3,12,68,388]{3,2,1,0:T(8,128)S(1)} %select_maximum_fusion.6, f32[3,12,66,384]{3,2,1,0:T(8,128)} %get-tuple-element.106, f32[3,12,66,384]{3,2,1,0:T(8,128)} %get-tuple-element.105, f32[3,10,64,384]{3,2,1,0:T(8,128)} %get-tuple-element.121, f32[3,10,64,384]{3,2,1,0:T(8,128)S(1)} %get-tuple-element.120, ...), kind=kLoop, calls=%fused_computation.57 | loop fusion | flops 16515072 | bytes 35389440 | tf_op jit(solution)/shard_map/sub | solution.py:83
  335.2 3.1 multiply_bitcast_fusion.1
  338.3 1.8 fusion.74
  342.4 1.7 collective-permute-start.15
  344.1 3.3 collective-permute-start.12
  347.5 2.7 convolution_bitcast_fusion.2
  350.2 14.7 %all-reduce.21 = (f32[4,384]{1,0:T(4,128)S(1)}, f32[100]{0:T(128)S(1)}) all-reduce(f32[4,384]{1,0:T(4,128)S(1)} %pad_maximum_fusion.15, f32[100]{0:T(128)S(1)} %convolution_bitcast_fusion.2), channel_id=1, replica_groups=mesh['gx_0'=4,'gx_1'=4,'gy_0'=4,'gy_1'=2] {'gx_0'}, use_global_device_ids=true, to_apply=%region_58.59 | all-reduce | flops 1636 | bytes 13088 | tf_op jit(solution)/shard_map/psum | solution.py:24
  364.9 7.2 %all-reduce.17 = (f32[4,384]{1,0:T(4,128)S(1)}, f32[100]{0:T(128)S(1)}) all-reduce(f32[4,384]{1,0:T(4,128)S(1)} %get-tuple-element.59, f32[100]{0:T(128)S(1)} %get-tuple-element.60), channel_id=1, replica_groups=mesh['gx_0'=4,'gx_1'=4,'gy_0'=4,'gy_1'=2] {'gx_1'}, use_global_device_ids=true, to_apply=%region_59.60 | all-reduce | flops 1636 | bytes 13088 | tf_op jit(solution)/shard_map/psum | solution.py:24
  372.1 9.2 %all-reduce.13 = (f32[4,384]{1,0:T(4,128)S(1)}, f32[100]{0:T(128)S(1)}) all-reduce(f32[4,384]{1,0:T(4,128)S(1)} %get-tuple-element.50, f32[100]{0:T(128)S(1)} %get-tuple-element.51), channel_id=1, replica_groups=mesh['gx_0'=4,'gx_1'=4,'gy_0'=4,'gy_1'=2] {'gy_0'}, use_global_device_ids=true, to_apply=%region_60.61 | all-reduce | flops 1636 | bytes 13088 | tf_op jit(solution)/shard_map/psum | solution.py:24
  381.3 6.7 %all-reduce.25 = (f32[4,384]{1,0:T(4,128)S(1)}, f32[100]{0:T(128)S(1)}) all-reduce(f32[4,384]{1,0:T(4,128)S(1)} %get-tuple-element.41, f32[100]{0:T(128)S(1)} %get-tuple-element.42), channel_id=1, replica_groups=mesh['gx_0'=4,'gx_1'=4,'gy_0'=4,'gy_1'=2] {'gy_1'}, use_global_device_ids=true, to_apply=%region_61.62 | all-reduce | flops 1636 | bytes 13088 | tf_op jit(solution)/shard_map/psum | solution.py:24
  390.7 2.7 dynamic_update_slice.60
  393.4 1.5 bitcast_subtract_fusion.2
  394.9 2.7 dynamic_update_slice.61
  399.0 2.8 dynamic_update_slice.62
  403.3 2.7 dynamic_update_slice.63
  408.4 7.7 %select_maximum_fusion = f32[3,12,68,388]{3,2,1,0:T(8,128)S(1)} fusion(f32[3,12,2,384]{3,2,1,0:T(2,128)S(1)} %pad.47, f32[3,12,2,384]{3,2,1,0:T(2,128)S(1)} %pad.48, f32[3,2,64,384]{3,2,1,0:T(8,128)S(1)} %collective-permute-done.12, f32[3,2,64,384]{3,2,1,0:T(8,128)} %collective-permute-done.13, f32[1,8,64,384]{3,2,1,0:T(8,128)S(1)} %get-tuple-element.118, ...), kind=kLoop, calls=%fused_computation.2 | loop fusion | flops 15197184 | bytes 7559424 | tf_op jit(solution)/shard_map/concatenate | solution.py:43
  416.1 4.8 %pad_maximum_fusion.2 = (f32[3,12,66,384]{3,2,1,0:T(8,128)}, f32[3,12,66,384]{3,2,1,0:T(8,128)}) fusion(f32[3,12,2,384]{3,2,1,0:T(2,128)S(1)} %pad.47, f32[3,2,64,384]{3,2,1,0:T(8,128)S(1)} %collective-permute-done.12, f32[1,8,64,384]{3,2,1,0:T(8,128)S(1)} %get-tuple-element.118, f32[1,8,64,384]{3,2,1,0:T(8,128)S(1)} %get-tuple-element.81, ...), kind=kLoop, calls=%fused_computation.31 | loop fusion | flops 9123840 | bytes 11059200 | tf_op jit(solution)/shard_map/concatenate | solution.py:43
  422.4 7.5 %fusion.6 = f32[3,8,64,384]{3,2,1,0:T(8,128)} fusion(f32[3,12,68,388]{3,2,1,0:T(8,128)S(1)} %select_maximum_fusion, f32[3,12,66,384]{3,2,1,0:T(8,128)} %get-tuple-element.104, f32[3,12,66,384]{3,2,1,0:T(8,128)} %get-tuple-element.103, f32[3,10,64,384]{3,2,1,0:T(8,128)S(1)} %get-tuple-element.112, f32[3,10,64,384]{3,2,1,0:T(8,128)S(1)} %get-tuple-element.111, ...), kind=kLoop, calls=%fused_computation.45 | loop fusion | flops 16515072 | bytes 35389440 | tf_op jit(solution)/shard_map/sub | solution.py:83
  429.9 1.7 fusion.45
  432.9 1.6 pad_maximum_fusion.11
  (267 shorter events, 55.9 us)
Async XLA Ops:
  0.6 12.7 %copy-start = (f32[3,8,64,384]{3,2,1,0:T(8,128)S(1)}, f32[3,8,64,384]{3,2,1,0:T(8,128)}, u32[]{:S(2)}) copy-start(f32[3,8,64,384]{3,2,1,0:T(8,128)} %param.8) | copy-start | bytes 7077892
  1.9 143.4 %collective-permute-start.2 = (f32[3,8,2,384]{3,2,1,0:T(2,128)S(1)}, f32[3,8,2,384]{3,2,1,0:T(2,128)S(1)}, u32[]{:S(2)}, u32[]{:S(2)}) collective-permute-start(f32[3,8,2,384]{3,2,1,0:T(2,128)S(1)} %get-tuple-element.143), channel_id=1, source_target_pairs={{1,0},{2,1},{3,2},{4,3},{5,4},{6,5},{7,6},{0,7},{9,8},{10,9},{11,1... | collective-permute-start | bytes 221192 | tf_op jit(solution)/shard_map/ppermute | solution.py:37
  5.6 139.7 %collective-permute-start.1 = (f32[3,2,64,384]{3,2,1,0:T(8,128)}, f32[3,2,64,384]{3,2,1,0:T(8,128)}, u32[]{:S(2)}, u32[]{:S(2)}) collective-permute-start(f32[3,2,64,384]{3,2,1,0:T(8,128)} %get-tuple-element.145), channel_id=1, source_target_pairs={{0,8},{8,16},{16,24},{24,32},{32,40},{40,48},{48,56},{56,64},{64,7... | collective-permute-start | bytes 1769480 | tf_op jit(solution)/shard_map/ppermute | solution.py:36
  7.4 140.1 %collective-permute-start = (f32[3,2,64,384]{3,2,1,0:T(8,128)}, f32[3,2,64,384]{3,2,1,0:T(8,128)}, u32[]{:S(2)}, u32[]{:S(2)}) collective-permute-start(f32[3,2,64,384]{3,2,1,0:T(8,128)} %get-tuple-element.144), channel_id=1, source_target_pairs={{8,0},{16,8},{24,16},{32,24},{40,32},{48,40},{56,48},{64,56},{72,6... | collective-permute-start | bytes 1769480 | tf_op jit(solution)/shard_map/ppermute | solution.py:37
  12.0 133.3 %collective-permute-start.3 = (f32[3,8,2,384]{3,2,1,0:T(2,128)S(1)}, f32[3,8,2,384]{3,2,1,0:T(2,128)S(1)}, u32[]{:S(2)}, u32[]{:S(2)}) collective-permute-start(f32[3,8,2,384]{3,2,1,0:T(2,128)S(1)} %get-tuple-element.142), channel_id=1, source_target_pairs={{0,1},{1,2},{2,3},{3,4},{4,5},{5,6},{6,7},{7,0},{8,9},{9,10},{10,1... | collective-permute-start | bytes 221192 | tf_op jit(solution)/shard_map/ppermute | solution.py:36
  14.8 23.9 %copy-start.29 = (f32[1,4,16,128]{3,2,1,0:T(8,128)S(1)}, f32[1,4,16,128]{3,2,1,0:T(8,128)}, u32[]{:S(2)}) copy-start(f32[1,4,16,128]{3,2,1,0:T(8,128)} %param.12) | copy-start | bytes 98308
  14.8 24.0 %copy-start.54 = (s32[1,4]{1,0:T(1,128)S(1)}, s32[1,4]{1,0:T(1,128)}, u32[]{:S(2)}) copy-start(s32[1,4]{1,0:T(1,128)} %param.10) | copy-start | bytes 52
  14.8 58.3 %copy-start.34 = (f32[2,384]{1,0:T(2,128)S(1)}, f32[2,384]{1,0:T(2,128)}, u32[]{:S(2)}) copy-start(f32[2,384]{1,0:T(2,128)} %param.9) | copy-start | bytes 9220
  14.8 58.4 %copy-start.57 = (f32[1,4]{1,0:T(1,128)S(1)}, f32[1,4]{1,0:T(1,128)}, u32[]{:S(2)}) copy-start(f32[1,4]{1,0:T(1,128)} %param.15) | copy-start | bytes 52
  14.9 121.6 %copy-start.53 = (s32[100]{0:T(128)S(1)}, s32[100]{0:T(128)}, u32[]{:S(2)}) copy-start(s32[100]{0:T(128)} %param.13) | copy-start | bytes 1204
  14.9 121.8 %copy-start.41 = (s32[100]{0:T(128)S(1)}, s32[100]{0:T(128)}, u32[]{:S(2)}) copy-start(s32[100]{0:T(128)} %param.14) | copy-start | bytes 1204
  72.6 64.0 %copy-start.47 = (f32[100]{0:T(128)}, f32[100]{0:T(128)S(1)}, u32[]{:S(2)}) copy-start(f32[100]{0:T(128)S(1)} %get-tuple-element.76) | copy-start | bytes 1204
  136.6 10.9 %copy-start.59 = (s32[100]{0:T(128)}, s32[100]{0:T(128)S(1)}, u32[]{:S(2)}) copy-start(s32[100]{0:T(128)S(1)} %convert_reduce_fusion) | copy-start | bytes 1204
  136.9 5.9 %copy-start.44 = (f32[100]{0:T(128)}, f32[100]{0:T(128)S(1)}, u32[]{:S(2)}) copy-start(f32[100]{0:T(128)S(1)} %fusion.40) | copy-start | bytes 1204
  142.7 4.8 %copy-start.61 = (pred[100]{0:T(512)(128)(4,1)}, pred[100]{0:T(512)(128)(4,1)S(1)}, u32[]{:S(2)}) copy-start(pred[100]{0:T(512)(128)(4,1)S(1)} %broadcast_compare_fusion) | copy-start | bytes 304
  144.5 3.0 copy-start.21
  145.3 3.9 copy-start.30
  145.4 3.8 copy-start.31
  147.5 4.4 %copy-start.16 = (f32[3,10,64,384]{3,2,1,0:T(8,128)}, f32[3,10,64,384]{3,2,1,0:T(8,128)S(1)}, u32[]{:S(2)}) copy-start(f32[3,10,64,384]{3,2,1,0:T(8,128)S(1)} %get-tuple-element.141) | copy-start | bytes 8847364
  163.4 74.4 %copy-start.1 = (f32[8,64,384]{2,1,0:T(8,128)}, f32[8,64,384]{2,1,0:T(8,128)S(1)}, u32[]{:S(2)}) copy-start(f32[8,64,384]{2,1,0:T(8,128)S(1)} %get-tuple-element.99) | copy-start | bytes 2359300
  164.4 37.0 %copy-start.48 = (f32[100]{0:T(128)S(1)}, f32[100]{0:T(128)}, u32[]{:S(2)}) copy-start(f32[100]{0:T(128)} %copy-done.47) | copy-start | bytes 1204
  164.4 37.0 %copy-start.42 = (s32[100]{0:T(128)S(1)}, s32[100]{0:T(128)}, u32[]{:S(2)}) copy-start(s32[100]{0:T(128)} %param.14) | copy-start | bytes 1204
  164.4 37.0 %copy-start.45 = (f32[100]{0:T(128)S(1)}, f32[100]{0:T(128)}, u32[]{:S(2)}) copy-start(f32[100]{0:T(128)} %copy-done.44) | copy-start | bytes 1204
  164.4 37.0 %copy-start.55 = (s32[1,4]{1,0:T(1,128)S(1)}, s32[1,4]{1,0:T(1,128)}, u32[]{:S(2)}) copy-start(s32[1,4]{1,0:T(1,128)} %param.10) | copy-start | bytes 52
  198.0 21.8 %copy-start.32 = (f32[4,384]{1,0:T(4,128)}, f32[4,384]{1,0:T(4,128)S(1)}, u32[]{:S(2)}) copy-start(f32[4,384]{1,0:T(4,128)S(1)} %broadcast_multiply_fusion.5) | copy-start | bytes 18436
  198.0 21.8 %collective-permute-start.6 = (f32[3,8,2,384]{3,2,1,0:T(2,128)S(1)}, f32[3,8,2,384]{3,2,1,0:T(2,128)S(1)}, u32[]{:S(2)}, u32[]{:S(2)}) collective-permute-start(f32[3,8,2,384]{3,2,1,0:T(2,128)S(1)} %get-tuple-element.133), channel_id=1, source_target_pairs={{1,0},{2,1},{3,2},{4,3},{5,4},{6,5},{7,6},{0,7},{9,8},{10,9},{11,1... | collective-permute-start | bytes 221192 | tf_op jit(solution)/shard_map/ppermute | solution.py:37
  198.4 21.5 %collective-permute-start.7 = (f32[3,8,2,384]{3,2,1,0:T(2,128)S(1)}, f32[3,8,2,384]{3,2,1,0:T(2,128)S(1)}, u32[]{:S(2)}, u32[]{:S(2)}) collective-permute-start(f32[3,8,2,384]{3,2,1,0:T(2,128)S(1)} %get-tuple-element.132), channel_id=1, source_target_pairs={{0,1},{1,2},{2,3},{3,4},{4,5},{5,6},{6,7},{7,0},{8,9},{9,10},{10,1... | collective-permute-start | bytes 221192 | tf_op jit(solution)/shard_map/ppermute | solution.py:36
  199.8 20.2 %collective-permute-start.4 = (f32[3,2,64,384]{3,2,1,0:T(8,128)}, f32[3,2,64,384]{3,2,1,0:T(8,128)}, u32[]{:S(2)}, u32[]{:S(2)}) collective-permute-start(f32[3,2,64,384]{3,2,1,0:T(8,128)} %get-tuple-element.131), channel_id=1, source_target_pairs={{8,0},{16,8},{24,16},{32,24},{40,32},{48,40},{56,48},{64,56},{72,6... | collective-permute-start | bytes 1769480 | tf_op jit(solution)/shard_map/ppermute | solution.py:37
  200.8 19.2 %collective-permute-start.5 = (f32[3,2,64,384]{3,2,1,0:T(8,128)}, f32[3,2,64,384]{3,2,1,0:T(8,128)}, u32[]{:S(2)}, u32[]{:S(2)}) collective-permute-start(f32[3,2,64,384]{3,2,1,0:T(8,128)} %get-tuple-element.130), channel_id=1, source_target_pairs={{0,8},{8,16},{16,24},{24,32},{32,40},{40,48},{48,56},{56,64},{64,7... | collective-permute-start | bytes 1769480 | tf_op jit(solution)/shard_map/ppermute | solution.py:36
  219.9 28.6 %copy-start.36 = (f32[384]{0:T(512)}, f32[384]{0:T(512)S(1)}, u32[]{:S(2)}) copy-start(f32[384]{0:T(512)S(1)} %get-tuple-element.38) | copy-start | bytes 4612
  233.8 4.0 copy-start.28
  246.9 3.3 copy-start.19
  248.4 5.1 %copy-start.3 = (f32[1,8,64,384]{3,2,1,0:T(8,128)}, f32[1,8,64,384]{3,2,1,0:T(8,128)S(1)}, u32[]{:S(2)}) copy-start(f32[1,8,64,384]{3,2,1,0:T(8,128)S(1)} %get-tuple-element.87) | copy-start | bytes 2359300
  248.4 5.1 %copy-start.5 = (f32[1,8,64,384]{3,2,1,0:T(8,128)}, f32[1,8,64,384]{3,2,1,0:T(8,128)S(1)}, u32[]{:S(2)}) copy-start(f32[1,8,64,384]{3,2,1,0:T(8,128)S(1)} %get-tuple-element.127) | copy-start | bytes 2359300
  253.8 35.7 %copy-start.35 = (f32[2,384]{1,0:T(2,128)S(1)}, f32[2,384]{1,0:T(2,128)}, u32[]{:S(2)}) copy-start(f32[2,384]{1,0:T(2,128)} %param.9) | copy-start | bytes 9220
  253.8 39.2 %copy-start.49 = (f32[100]{0:T(128)S(1)}, f32[100]{0:T(128)}, u32[]{:S(2)}) copy-start(f32[100]{0:T(128)} %copy-done.47) | copy-start | bytes 1204
  253.8 39.1 %copy-start.43 = (s32[100]{0:T(128)S(1)}, s32[100]{0:T(128)}, u32[]{:S(2)}) copy-start(s32[100]{0:T(128)} %param.14) | copy-start | bytes 1204
  253.8 39.1 %copy-start.46 = (f32[100]{0:T(128)S(1)}, f32[100]{0:T(128)}, u32[]{:S(2)}) copy-start(f32[100]{0:T(128)} %copy-done.44) | copy-start | bytes 1204
  253.8 39.1 %copy-start.51 = (f32[100]{0:T(128)S(1)}, f32[100]{0:T(128)}, u32[]{:S(2)}) copy-start(f32[100]{0:T(128)} %copy-done.50) | copy-start | bytes 1204
  253.9 57.1 %copy-start.4 = (f32[1,8,64,384]{3,2,1,0:T(8,128)S(1)}, f32[1,8,64,384]{3,2,1,0:T(8,128)}, u32[]{:S(2)}) copy-start(f32[1,8,64,384]{3,2,1,0:T(8,128)} %copy-done.3) | copy-start | bytes 2359300
  253.9 57.1 %copy-start.6 = (f32[1,8,64,384]{3,2,1,0:T(8,128)S(1)}, f32[1,8,64,384]{3,2,1,0:T(8,128)}, u32[]{:S(2)}) copy-start(f32[1,8,64,384]{3,2,1,0:T(8,128)} %copy-done.5) | copy-start | bytes 2359300
  289.5 21.4 %collective-permute-start.10 = (f32[3,8,2,384]{3,2,1,0:T(2,128)S(1)}, f32[3,8,2,384]{3,2,1,0:T(2,128)S(1)}, u32[]{:S(2)}, u32[]{:S(2)}) collective-permute-start(f32[3,8,2,384]{3,2,1,0:T(2,128)S(1)} %get-tuple-element.125), channel_id=1, source_target_pairs={{1,0},{2,1},{3,2},{4,3},{5,4},{6,5},{7,6},{0,7},{9,8},{10,9},{11,1... | collective-permute-start | bytes 221192 | tf_op jit(solution)/shard_map/ppermute | solution.py:37
  289.9 21.1 %collective-permute-start.11 = (f32[3,8,2,384]{3,2,1,0:T(2,128)S(1)}, f32[3,8,2,384]{3,2,1,0:T(2,128)S(1)}, u32[]{:S(2)}, u32[]{:S(2)}) collective-permute-start(f32[3,8,2,384]{3,2,1,0:T(2,128)S(1)} %get-tuple-element.124), channel_id=1, source_target_pairs={{0,1},{1,2},{2,3},{3,4},{4,5},{5,6},{6,7},{7,0},{8,9},{9,10},{10,1... | collective-permute-start | bytes 221192 | tf_op jit(solution)/shard_map/ppermute | solution.py:36
  291.3 19.7 %collective-permute-start.8 = (f32[3,2,64,384]{3,2,1,0:T(8,128)}, f32[3,2,64,384]{3,2,1,0:T(8,128)S(1)}, u32[]{:S(2)}, u32[]{:S(2)}) collective-permute-start(f32[3,2,64,384]{3,2,1,0:T(8,128)} %get-tuple-element.123), channel_id=1, source_target_pairs={{8,0},{16,8},{24,16},{32,24},{40,32},{48,40},{56,48},{64,56},{72,6... | collective-permute-start | bytes 1769480 | tf_op jit(solution)/shard_map/ppermute | solution.py:37
  291.3 19.7 %collective-permute-start.9 = (f32[3,2,64,384]{3,2,1,0:T(8,128)}, f32[3,2,64,384]{3,2,1,0:T(8,128)}, u32[]{:S(2)}, u32[]{:S(2)}) collective-permute-start(f32[3,2,64,384]{3,2,1,0:T(8,128)} %get-tuple-element.122), channel_id=1, source_target_pairs={{0,8},{8,16},{16,24},{24,32},{32,40},{40,48},{48,56},{56,64},{64,7... | collective-permute-start | bytes 1769480 | tf_op jit(solution)/shard_map/ppermute | solution.py:36
  323.6 3.0 copy-start.27
  326.5 8.6 %copy-start.7 = (f32[1,8,64,384]{3,2,1,0:T(8,128)S(1)}, f32[1,8,64,384]{3,2,1,0:T(8,128)}, u32[]{:S(2)}) copy-start(f32[1,8,64,384]{3,2,1,0:T(8,128)} %copy-done.5) | copy-start | bytes 2359300
  335.1 3.2 copy-start.14
  335.1 3.2 copy-start.18
  335.1 3.2 copy-start.23
  335.1 3.2 copy-start.24
  335.1 3.2 copy-start.37
  340.4 65.6 %copy-start.58 = (f32[1,4]{1,0:T(1,128)S(1)}, f32[1,4]{1,0:T(1,128)}, u32[]{:S(2)}) copy-start(f32[1,4]{1,0:T(1,128)} %param.15) | copy-start | bytes 52
  340.4 65.6 %copy-start.60 = (s32[100]{0:T(128)S(1)}, s32[100]{0:T(128)}, u32[]{:S(2)}) copy-start(s32[100]{0:T(128)} %copy-done.59) | copy-start | bytes 1204
  340.4 65.6 %copy-start.62 = (pred[100]{0:T(512)(128)(4,1)S(1)}, pred[100]{0:T(512)(128)(4,1)}, u32[]{:S(2)}) copy-start(pred[100]{0:T(512)(128)(4,1)} %copy-done.61) | copy-start | bytes 304
  340.4 65.6 %copy-start.63 = (f32[4]{0:T(128)S(1)}, f32[4]{0:T(128)}, u32[]{:S(2)}) copy-start(f32[4]{0:T(128)} %convert_reduce_fusion.1) | copy-start | bytes 52
  340.5 67.1 %copy-start.33 = (f32[4,384]{1,0:T(4,128)S(1)}, f32[4,384]{1,0:T(4,128)}, u32[]{:S(2)}) copy-start(f32[4,384]{1,0:T(4,128)} %copy-done.32) | copy-start | bytes 18436
  340.5 67.1 %copy-start.39 = (f32[1,384]{1,0:T(1,128)S(1)}, f32[1,384]{1,0:T(1,128)}, u32[]{:S(2)}) copy-start(f32[1,384]{1,0:T(1,128)} %fusion.105) | copy-start | bytes 4612
  340.5 67.1 %copy-start.40 = (f32[1,384]{1,0:T(1,128)S(1)}, f32[1,384]{1,0:T(1,128)}, u32[]{:S(2)}) copy-start(f32[1,384]{1,0:T(1,128)} %fusion.104) | copy-start | bytes 4612
  342.4 65.8 %collective-permute-start.14 = (f32[3,8,2,384]{3,2,1,0:T(2,128)S(1)}, f32[3,8,2,384]{3,2,1,0:T(2,128)S(1)}, u32[]{:S(2)}, u32[]{:S(2)}) collective-permute-start(f32[3,8,2,384]{3,2,1,0:T(2,128)S(1)} %get-tuple-element.116), channel_id=1, source_target_pairs={{1,0},{2,1},{3,2},{4,3},{5,4},{6,5},{7,6},{0,7},{9,8},{10,9},{11,1... | collective-permute-start | bytes 221192 | tf_op jit(solution)/shard_map/ppermute | solution.py:37
  342.4 65.9 %collective-permute-start.15 = (f32[3,8,2,384]{3,2,1,0:T(2,128)S(1)}, f32[3,8,2,384]{3,2,1,0:T(2,128)S(1)}, u32[]{:S(2)}, u32[]{:S(2)}) collective-permute-start(f32[3,8,2,384]{3,2,1,0:T(2,128)S(1)} %get-tuple-element.115), channel_id=1, source_target_pairs={{0,1},{1,2},{2,3},{3,4},{4,5},{5,6},{6,7},{7,0},{8,9},{9,10},{10,1... | collective-permute-start | bytes 221192 | tf_op jit(solution)/shard_map/ppermute | solution.py:36
  344.1 64.2 %collective-permute-start.12 = (f32[3,2,64,384]{3,2,1,0:T(8,128)}, f32[3,2,64,384]{3,2,1,0:T(8,128)S(1)}, u32[]{:S(2)}, u32[]{:S(2)}) collective-permute-start(f32[3,2,64,384]{3,2,1,0:T(8,128)} %get-tuple-element.114), channel_id=1, source_target_pairs={{8,0},{16,8},{24,16},{32,24},{40,32},{48,40},{56,48},{64,56},{72,6... | collective-permute-start | bytes 1769480 | tf_op jit(solution)/shard_map/ppermute | solution.py:37
  347.5 60.9 %collective-permute-start.13 = (f32[3,2,64,384]{3,2,1,0:T(8,128)}, f32[3,2,64,384]{3,2,1,0:T(8,128)}, u32[]{:S(2)}, u32[]{:S(2)}) collective-permute-start(f32[3,2,64,384]{3,2,1,0:T(8,128)} %get-tuple-element.113), channel_id=1, source_target_pairs={{0,8},{8,16},{16,24},{24,32},{32,40},{40,48},{48,56},{56,64},{64,7... | collective-permute-start | bytes 1769480 | tf_op jit(solution)/shard_map/ppermute | solution.py:36
  388.1 28.0 %copy-start.52 = (f32[100]{0:T(128)}, f32[100]{0:T(128)S(1)}, u32[]{:S(2)}) copy-start(f32[100]{0:T(128)S(1)} %get-tuple-element.77) | copy-start | bytes 1204
  (16 other events, 30.8 us)
where the time goes:
time: 441 us; the launch traced here: 435 us
  blocking collectives  192 us (44%)
  other arithmetic  126 us (29%)
  local copies, waits for them, and re-layouts  57.7 us (13%)
  between operations  24.7 us (6%)
  starting transfers between devices  21 us (5%)
  matrix products  12.6 us (3%)
    psum x16, blocking collectives, by_axis(): shard = lax.psum(shard, axis)  129 us
    all_gather x1, blocking collectives, local(): state_all = lax.all_gather(controller_state[0], GX_GY, axis=0, tiled=True)  63.1 us
    concatenate x10, other arithmetic, padded_2(): jnp.concatenate([jnp.pad(low, around), shard, jnp.pad(high, around)], axi...  49.4 us
    dynamic_update_slice x16, local copies, waits for them, and re-layouts, local(): lax.dynamic_update_slice(force_field, previous - slot_factor[slot_index]...  36.8 us
    sub x4, other arithmetic, tendency(): return VISCOSITY * laplacian - advection  33.3 us
    sub x16, other arithmetic, local(): previous - slot_factor[slot_index] * weights_local[slot_index][None]  17.7 us
    ppermute x8, starting transfers between devices, padded_2(): lax.ppermute(first, axis, [(b, a) for a, b in up])  11 us
    dot_general x4, matrix products, local(): numerator_part = jnp.dot(contribution, slot_onehot, precision=HIGHEST)  10.8 us
  transfers between devices with their start and end apart: 16, of which 0 were waited for; matrix products, arithmetic and copies ran while one was open for 18% of the time, Pallas kernels for 0%

commit v1 on v0

v1 whole, which is shorter than its diff:
```python
import functools

import jax
import jax.numpy as jnp
from jax import lax
from jax.experimental import pallas as pl
from jax.experimental.pallas import tpu as pltpu
from jax.sharding import Mesh
from jax.sharding import PartitionSpec as P

STEPS = 4
GX = ("gx_0", "gx_1")
GY = ("gy_0", "gy_1")
GX_GY = ("gx_0", "gx_1", "gy_0", "gy_1")
CHIPS = ("gx_0", "gx_1", "gy_0")

LANES = 128
ROWS = 16
ROW_U, ROW_V, ROW_W, ROW_UW, ROW_NUM, ROW_AREA, ROW_INT = 0, 3, 6, 9, 12, 13, 14
CHUNK = 16


def placed_spec(space):
    return pl.BlockSpec(memory_space=space)


VM = pltpu.VMEM
SM = pltpu.SMEM
ANY = pl.ANY


def sums_kernel(starts, ids, velocity, weight, integral0, payload, planes, field, sem, *, copies):
    _, nx, ny, nz = velocity.shape
    tiles = nz // LANES
    slots, tile_y, tile_z = weight.shape
    load = pltpu.make_async_copy(velocity, field, sem)
    load.start()
    for s in range(slots):
        tile = jnp.concatenate(
            [weight[s], jnp.zeros((tile_y, nz - tile_z), jnp.float32)], axis=1
        )
        tile = pltpu.roll(tile, starts[2, s], axis=1)
        plane = jnp.concatenate([tile, jnp.zeros((ny - tile_y, nz), jnp.float32)], axis=0)
        planes[s] = pltpu.roll(plane, starts[1, s], axis=0)
    load.wait()

    def add_plane(i, carry):
        out = []
        for t in range(tiles):
            lanes = slice(t * LANES, (t + 1) * LANES)
            u = field[0, i, :, lanes].reshape(ny // 8, 8, LANES)
            v = field[1, i, :, lanes].reshape(ny // 8, 8, LANES)
            w = field[2, i, :, lanes].reshape(ny // 8, 8, LANES)
            out.append(
                (
                    carry[t][0] + jnp.sum(u, axis=0),
                    carry[t][1] + jnp.sum(v, axis=0),
                    carry[t][2] + jnp.sum(w, axis=0),
                    carry[t][3] + jnp.sum(u * w, axis=0),
                )
            )
        return tuple(out)

    zero = jnp.zeros((8, LANES), jnp.float32)
    sums = lax.fori_loop(0, nx, add_plane, ((zero,) * 4,) * tiles)
    rows = [None] * ROWS
    for q, base in enumerate((ROW_U, ROW_V, ROW_W, ROW_UW)):
        for t in range(tiles):
            rows[base + t] = jnp.sum(sums[t][q], axis=0, keepdims=True)
    lane = lax.broadcasted_iota(jnp.int32, (1, LANES), 1)
    numerator = jnp.zeros((1, LANES), jnp.float32)
    area = jnp.zeros((1, LANES), jnp.float32)
    for s in range(slots):
        mine = lane == ids[0, s]
        seen = jnp.sum(planes[s] * field[0, starts[0, s]], keepdims=True)
        total = jnp.sum(weight[s], keepdims=True)
        numerator = numerator + jnp.where(mine, seen, 0.0)
        area = area + jnp.where(mine, total, 0.0)
    rows[ROW_NUM] = numerator
    rows[ROW_AREA] = area
    rows[ROW_INT] = integral0[...]
    rows[ROWS - 1] = jnp.zeros((1, LANES), jnp.float32)
    full = jnp.concatenate(rows, axis=0)
    for c in range(copies):
        payload[c] = full


def step_kernel(
    starts, ids, velocity, x_low, x_high, y_low, y_high, reduced, planes, target, terms, state,
    *rest, cells, last, first, turbines, copies,
):
    if last:
        velocity_out, state_out = rest[:2]
        scratch = rest[2:]
    else:
        velocity_out, xs_low, xs_high, ys_low, ys_high, payload, state_out = rest[:7]
        scratch = rest[7:]
    padded, field, sums, sems = scratch
    _, nx, ny, nz = velocity.shape
    tiles = nz // LANES
    slots = planes.shape[0]
    loads = []
    for t in range(tiles):
        lanes = pl.ds(t * LANES, LANES)
        loads.append(
            pltpu.make_async_copy(
                velocity.at[:, :, :, lanes],
                padded.at[:, pl.ds(2, nx), t, pl.ds(8, ny), :],
                sems.at[3 * t],
            )
        )
        loads.append(
            pltpu.make_async_copy(
                x_low.at[:, :, :, lanes],
                padded.at[:, pl.ds(0, 2), t, pl.ds(8, ny), :],
                sems.at[3 * t + 1],
            )
        )
        loads.append(
            pltpu.make_async_copy(
                x_high.at[:, :, :, lanes],
                padded.at[:, pl.ds(nx + 2, 2), t, pl.ds(8, ny), :],
                sems.at[3 * t + 2],
            )
        )
    for load in loads:
        load.start()

    lane = lax.broadcasted_iota(jnp.int32, (1, LANES), 1)
    total = reduced[0] + reduced[1]
    means = total[0:12] * (1.0 / cells)
    if first:
        area = total[ROW_AREA : ROW_AREA + 1]
        integral = total[ROW_INT : ROW_INT + 1]
        profiles = jnp.zeros((12, LANES), jnp.float32)
    else:
        area = state[13:14]
        integral = state[12:13]
        profiles = state[0:12]
    live = lane < turbines
    disc_speed = total[ROW_NUM : ROW_NUM + 1] / jnp.where(live, area, 1.0)
    speed_error = disc_speed - terms[0:1]
    integral = integral + 0.5 * speed_error
    thrust = 0.1 + 0.9 * jax.nn.sigmoid(terms[1:2] - 2.0 * speed_error - integral)
    factor = 0.5 * thrust * disc_speed * jnp.abs(disc_speed)
    product = jnp.concatenate(
        [jnp.zeros((9, LANES), jnp.float32), means[0:3] * means[6:9]], axis=0
    )
    state_out[0:12] = profiles + (means - product)
    state_out[12:13] = integral
    state_out[13:14] = area
    state_out[14:15] = thrust
    state_out[15:16] = jnp.zeros((1, LANES), jnp.float32)
    push = [0.1 * (target[r : r + 1] - means[r : r + 1]) for r in range(6)]
    forces = [
        -0.2 * jnp.sum(jnp.where(lane == ids[0, s], factor, 0.0), axis=1, keepdims=True)
        for s in range(slots)
    ]

    for c in range(3):
        for i in range(nx):
            for t in range(tiles):
                lanes = slice(t * LANES, (t + 1) * LANES)
                padded[c, i + 2, t, 6:8, :] = y_low[c, i, :, lanes]
                padded[c, i + 2, t, 8 + ny : 10 + ny, :] = y_high[c, i, :, lanes]
    for load in loads:
        load.wait()

    if not last:
        sums[...] = jnp.zeros(sums.shape, jnp.float32)
    wide = lax.broadcasted_iota(jnp.int32, (CHUNK, LANES), 1)
    edge = [wide < 1, wide < 2, wide >= LANES - 1, wide >= LANES - 2]

    def plane(i, carry):
        for y in range(0, ny, CHUNK):

            def at(c, t, dx, dy):
                return padded[c, i + 2 + dx, t, pl.ds(8 + y + dy, CHUNK), :]

            speed = [[at(c, t, 0, 0) for t in range(tiles)] for c in range(3)]
            new = [[None] * tiles for _ in range(3)]
            for c in range(3):
                centre = speed[c]
                up1 = [pltpu.roll(centre[t], 1, axis=1) for t in range(tiles)]
                up2 = [pltpu.roll(centre[t], 2, axis=1) for t in range(tiles)]
                dn1 = [pltpu.roll(centre[t], LANES - 1, axis=1) for t in range(tiles)]
                dn2 = [pltpu.roll(centre[t], LANES - 2, axis=1) for t in range(tiles)]
                for t in range(tiles):
                    f = centre[t]
                    below, above = t > 0, t < tiles - 1
                    zm1 = jnp.where(edge[0], up1[t - 1] if below else 0.0, up1[t])
                    zm2 = jnp.where(edge[1], up2[t - 1] if below else 0.0, up2[t])
                    zp1 = jnp.where(edge[2], dn1[t + 1] if above else 0.0, dn1[t])
                    zp2 = jnp.where(edge[3], dn2[t + 1] if above else 0.0, dn2[t])
                    xm1, xp1 = at(c, t, -1, 0), at(c, t, 1, 0)
                    ym1, yp1 = at(c, t, 0, -1), at(c, t, 0, 1)
                    grad_x = 8.0 * (xp1 - xm1) - (at(c, t, 2, 0) - at(c, t, -2, 0))
                    grad_y = 8.0 * (yp1 - ym1) - (at(c, t, 0, 2) - at(c, t, 0, -2))
                    grad_z = 8.0 * (zp1 - zm1) - (zp2 - zm2)
                    around = (xp1 + xm1) + (yp1 + ym1) + (zp1 + zm1)
                    moved = speed[0][t] * grad_x + speed[1][t] * grad_y + speed[2][t] * grad_z
                    result = 0.88 * f + (0.02 * around - (0.2 / 12.0) * moved)
                    if c < 2:
                        result = result + push[3 * c + t]
                    new[c][t] = result
                    field[c, i, y : y + CHUNK, t * LANES : (t + 1) * LANES] = result
            if not last:
                for t in range(tiles):
                    u, v, w = new[0][t], new[1][t], new[2][t]
                    for q, value in enumerate((u, v, w, u * w)):
                        part = value[0:8]
                        for r in range(8, CHUNK, 8):
                            part = part + value[r : r + 8]
                        sums[q, t] = sums[q, t] + part
        return carry

    lax.fori_loop(0, nx, plane, 0)

    for s in range(slots):
        i = starts[0, s]
        push_s = forces[s] * planes[s]
        field[0, i] = field[0, i] + push_s
        if not last:
            along = push_s * field[2, i]
            for t in range(tiles):
                lanes = slice(t * LANES, (t + 1) * LANES)
                sums[0, t] = sums[0, t] + jnp.sum(
                    push_s[:, lanes].reshape(ny // 8, 8, LANES), axis=0
                )
                sums[3, t] = sums[3, t] + jnp.sum(
                    along[:, lanes].reshape(ny // 8, 8, LANES), axis=0
                )

    stores = [pltpu.make_async_copy(field, velocity_out, sems.at[0])]
    if not last:
        stores.append(pltpu.make_async_copy(field.at[:, pl.ds(0, 2)], xs_low, sems.at[1]))
        stores.append(pltpu.make_async_copy(field.at[:, pl.ds(nx - 2, 2)], xs_high, sems.at[2]))
    for store in stores:
        store.start()
    if not last:
        ys_low[...] = field[:, :, 0:2, :]
        ys_high[...] = field[:, :, ny - 2 : ny, :]
        rows = []
        for q in range(4):
            for t in range(tiles):
                rows.append(jnp.sum(sums[q, t], axis=0, keepdims=True))
        numerator = jnp.zeros((1, LANES), jnp.float32)
        for s in range(slots):
            seen = jnp.sum(planes[s] * field[0, starts[0, s]], keepdims=True)
            numerator = numerator + jnp.where(lane == ids[0, s], seen, 0.0)
        rows.append(numerator)
        rows.append(jnp.zeros((3, LANES), jnp.float32))
        full = jnp.concatenate(rows, axis=0)
        for k in range(copies):
            payload[k] = full
    for store in stores:
        store.wait()


def first_sums(starts, ids, velocity, weight, integral0, copies):
    _, nx, ny, nz = velocity.shape
    return pl.pallas_call(
        functools.partial(sums_kernel, copies=copies),
        out_shape=(
            jax.ShapeDtypeStruct((copies, ROWS, LANES), jnp.float32),
            jax.ShapeDtypeStruct((weight.shape[0], ny, nz), jnp.float32),
        ),
        in_specs=[placed_spec(SM), placed_spec(SM), placed_spec(ANY), placed_spec(VM), placed_spec(VM)],
        out_specs=(placed_spec(VM), placed_spec(VM)),
        scratch_shapes=[pltpu.VMEM(velocity.shape, jnp.float32), pltpu.SemaphoreType.DMA(())],
        compiler_params=pltpu.CompilerParams(vmem_limit_bytes=24 * 2**20),
        name="first_sums",
    )(starts, ids, velocity, weight, integral0)


def one_step(starts, ids, velocity, halos, reduced, planes, target, terms, state, *, cells, last, first, turbines, copies):
    _, nx, ny, nz = velocity.shape
    x_low, x_high, y_low, y_high = halos
    f32 = jnp.float32
    outs = [jax.ShapeDtypeStruct(velocity.shape, f32)]
    specs = [placed_spec(ANY)]
    if not last:
        outs += [jax.ShapeDtypeStruct((3, 2, ny, nz), f32)] * 2
        specs += [placed_spec(ANY)] * 2
        outs += [jax.ShapeDtypeStruct((3, nx, 2, nz), f32)] * 2
        specs += [placed_spec(VM)] * 2
        outs += [jax.ShapeDtypeStruct((copies, ROWS, LANES), f32)]
        specs += [placed_spec(VM)]
    outs += [jax.ShapeDtypeStruct((16, LANES), f32)]
    specs += [placed_spec(VM)]
    return pl.pallas_call(
        functools.partial(
            step_kernel, cells=cells, last=last, first=first, turbines=turbines, copies=copies
        ),
        out_shape=tuple(outs),
        in_specs=[placed_spec(SM)] * 2 + [placed_spec(ANY)] * 3 + [placed_spec(VM)] * 7,
        out_specs=tuple(specs),
        scratch_shapes=[
            pltpu.VMEM((3, nx + 4, nz // LANES, ny + 16, LANES), f32),
            pltpu.VMEM(velocity.shape, f32),
            pltpu.VMEM((4, nz // LANES, 8, LANES), f32),
            pltpu.SemaphoreType.DMA((9,)),
        ],
        compiler_params=pltpu.CompilerParams(vmem_limit_bytes=32 * 2**20),
        name="one_step",
    )(starts, ids, velocity, x_low, x_high, y_low, y_high, reduced, planes, target, terms, state)


def exchange(edges):
    def shift(block, axis, by):
        n = lax.axis_size(axis)
        return lax.ppermute(block, axis, [(i, (i + by) % n) for i in range(n)])

    x_first, x_last, y_first, y_last = edges
    return (
        shift(x_last, GX, 1),
        shift(x_first, GX, -1),
        shift(y_last, GY, 1),
        shift(y_first, GY, -1),
    )


def reduce_all(payload):
    got = lax.all_to_all(payload, CHIPS, 0, 0, tiled=True)
    mine = jnp.sum(got, axis=0)
    other = lax.ppermute(mine, "gy_1", [(0, 1), (1, 0)])
    return jnp.stack([mine, other])


def owner_rank(turbine_owner):
    turbines = turbine_owner.shape[0]
    ids = jnp.arange(turbines, dtype=jnp.int32)
    same_owner = turbine_owner[:, None] == turbine_owner[None, :]
    earlier = ids[None, :] < ids[:, None]
    return jnp.sum((same_owner & earlier).astype(jnp.int32), axis=1)


def local(
    velocity, target_profile, disc_turbine, disc_start, disc_weight, turbine_owner, mode_flag,
    controller_state,
):
    blocks_x = lax.axis_size(GX)
    blocks_y = lax.axis_size(GY)
    device_me = lax.axis_index(GX) * blocks_y + lax.axis_index(GY)
    _, nx, ny, nz = velocity.shape
    turbines = mode_flag.shape[0]
    owned = controller_state.shape[1]
    cells = float(nx * blocks_x * ny * blocks_y)
    copies = lax.axis_size(CHIPS)
    starts = disc_start[:, 0, :]
    ids = disc_turbine

    rank = owner_rank(turbine_owner)
    mine_table = (turbine_owner[:, None] == device_me) & (
        rank[:, None] == jnp.arange(owned, dtype=jnp.int32)[None, :]
    )
    held = jnp.sum(jnp.where(mine_table, controller_state[0][None, :], 0.0), axis=1)
    spare = (0, LANES - turbines)
    integral0 = jnp.pad(held, spare)[None, :]
    rated = jnp.where(mode_flag == 0, 0.7, jnp.where(mode_flag == 1, 0.9, 1.1)).astype(jnp.float32)
    bias = jnp.where(mode_flag == 0, 1.0, jnp.where(mode_flag == 1, 0.0, -1.0)).astype(jnp.float32)
    terms = jnp.stack([jnp.pad(rated, spare), jnp.pad(bias, spare)])
    target = target_profile.reshape(2 * nz // LANES, LANES)

    edges = (
        velocity[:, 0:2],
        velocity[:, nx - 2 : nx],
        velocity[:, :, 0:2],
        velocity[:, :, ny - 2 : ny],
    )
    payload, planes = first_sums(starts, ids, velocity, disc_weight[0], integral0, copies)
    state = jnp.zeros((16, LANES), jnp.float32)
    for turn in range(STEPS):
        halos = exchange(edges)
        reduced = reduce_all(payload)
        out = one_step(
            starts, ids, velocity, halos, reduced, planes, target, terms, state,
            cells=cells, last=turn == STEPS - 1, first=turn == 0, turbines=turbines, copies=copies,
        )
        velocity, state = out[0], out[-1]
        if turn < STEPS - 1:
            edges, payload = out[1:5], out[5]
    profiles = state[0:12].reshape(4, nz) / STEPS
    integral = state[12, :turbines]
    thrust = state[14, :turbines]
    updated = jnp.sum(jnp.where(mine_table, integral[:, None], 0.0), axis=0)
    controller = jnp.where(jnp.any(mine_table, axis=0), updated, controller_state[0])
    return velocity, profiles, thrust, controller[None, :]


def solution(mesh):
    torus = Mesh(mesh.devices.reshape(4, 4, 4, 2), ("gx_0", "gx_1", "gy_0", "gy_1"))
    placed = (
        P(None, GX, GY, None),
        P(),
        P(GX_GY, None),
        P(None, GX_GY, None),
        P(GX_GY, None, None, None),
        P(),
        P(),
        P(GX_GY, None),
    )
    return jax.shard_map(
        local,
        mesh=torus,
        in_specs=placed,
        out_specs=(P(None, GX, GY, None), P(), P(), P(GX_GY, None)),
        check_vma=False,
    )
```

time: 441 us -> 174 us (0.39); the launches traced: 435 us -> 173 us
  blocking collectives: 192 us -> 0 us
  other arithmetic: 126 us -> 5.45 us
  waiting for transfers between devices: 0.04 us -> 56.9 us
  starting transfers between devices: 21 us -> 63.9 us
  local copies, waits for them, and re-layouts: 57.7 us -> 20.9 us
  Pallas kernels: 0 us -> 25.1 us
  between operations: 24.7 us -> 0.87 us
  matrix products: 12.6 us -> 0 us
    psum x16 -> x0, blocking collectives: 129 us -> none  [by_axis(): shard = lax.psum(shard, axis)]
    all_gather x1 -> x0, blocking collectives: 63.1 us -> none  [local(): state_all = lax.all_gather(controller_state[0], GX_GY, axis=0, tiled=True)]
    sub x24 -> x0, other arithmetic: 52.2 us -> none  [the longest x4 33.3 us: tendency(): return VISCOSITY * laplacian - advection]
    concatenate x10 -> x0, other arithmetic: 49.4 us -> none  [padded_2(): jnp.concatenate([jnp.pad(low, around), shard, jnp.pad(high, around)], axi...]
    dynamic_update_slice x16 -> x0, local copies, waits for them, and re-layouts: 36.8 us -> none  [local(): lax.dynamic_update_slice(force_field, previous - slot_factor[slot_index]...]
    all_to_all x0 -> x4, starting transfers between devices: none -> 31.7 us  [reduce_all(): got = lax.all_to_all(payload, CHIPS, 0, 0, tiled=True)]
    ppermute x16 -> x20, waiting for transfers between devices: 0.04 us -> 31.7 us  [the longest x16 30 us: shift(): return lax.ppermute(block, axis, [(i, (i + by) % n) for i in range(n)])]
    all_to_all x0 -> x4, waiting for transfers between devices: none -> 25.3 us  [reduce_all(): got = lax.all_to_all(payload, CHIPS, 0, 0, tiled=True)]
  transfers between devices with their start and end apart: 16 -> 24, of which waited for: 0 -> 18; matrix products, arithmetic and copies ran while one was open for 18% -> 2% of each run, Pallas kernels for 0% -> 0%
where the time goes in v1:
time: 174 us; the launch traced here: 173 us
  starting transfers between devices  63.9 us (37%)
  waiting for transfers between devices  56.9 us (33%)
  Pallas kernels  25.1 us (14%)
  local copies, waits for them, and re-layouts  20.9 us (12%)
  other arithmetic  5.45 us (3%)
    all_to_all x4, starting transfers between devices, reduce_all(): got = lax.all_to_all(payload, CHIPS, 0, 0, tiled=True)  31.7 us
    ppermute x16, waiting for transfers between devices, shift(): return lax.ppermute(block, axis, [(i, (i + by) % n) for i in range(n)])  30 us
    all_to_all x4, waiting for transfers between devices, reduce_all(): got = lax.all_to_all(payload, CHIPS, 0, 0, tiled=True)  25.3 us
    ppermute x16, starting transfers between devices, shift(): return lax.ppermute(block, axis, [(i, (i + by) % n) for i in range(n)])  23.5 us
    pallas_call x4, Pallas kernels, one_step(): pl.pallas_call(functools.partial(step_kernel, cells=cells, last=last, fir...  23 us
    unnamed x45, local copies, waits for them, and re-layouts  17.9 us
    ppermute x4, starting transfers between devices, reduce_all(): other = lax.ppermute(mine, 'gy_1', [(0, 1), (1, 0)])  8.72 us
  transfers between devices with their start and end apart: 24, of which 18 were waited for; matrix products, arithmetic and copies ran while one was open for 2% of the time, Pallas kernels for 0%

profile of v1, /device:TPU:1, one launch (start us, length us, event | category | flops | bytes accessed | tf_op | source)
XLA Modules:
  0.0 173.2 jit_solution(4936237074163698219)
XLA Ops:
  0.6 0.9 convert_reduce_fusion
  1.6 0.7 broadcast_compare_fusion
  2.2 0.7 select_reduce_fusion.1
  3.0 0.7 copy.14
  3.7 1.7 copy-done
  5.3 0.8 copy-done.10
  6.1 0.7 copy-done.11
  6.7 2.1 %first_sums.1 = (f32[64,16,128]{2,1,0:T(8,128)}, f32[4,64,384]{2,1,0:T(8,128)S(1)}) custom-call(s32[3,4]{1,0:T(4,128)S(1)} %bitcast.27, s32[1,4]{1,0:T(1,128)S(1)} %copy-done.11, f32[3,8,64,384]{3,2,1,0:T(8,128)S(1)} %copy-done, f32[4,16,128]{2,1,0:T(8,128)S(1)} %bitcast.32, f32[1,128]{1,0:T(1,128)S(1)} %pad_bitcast_fusion.2.integral0), custom_call_target="tpu_custom_call" | custom-call | tf_op jit(solution)/shard_map/first_sums/pallas_call | solution.py:262
  8.9 12.4 %all-to-all-start = ((f32[64,16,128]{2,1,0:T(8,128)}), f32[64,16,128]{2,1,0:T(8,128)}, u32[]{:S(2)}, u32[]{:S(2)}) async-start(f32[64,16,128]{2,1,0:T(8,128)} %get-tuple-element.29), calls=%async_computation | async-start | bytes 1048576 | tf_op jit(solution)/shard_map/all_to_all | solution.py:324
  21.3 1.1 fusion.4
  22.3 0.9 collective-permute-start
  23.3 3.8 %collective-permute-start.1 = (f32[3,2,64,384]{3,2,1,0:T(8,128)}, f32[3,2,64,384]{3,2,1,0:T(8,128)}, u32[]{:S(2)}, u32[]{:S(2)}) collective-permute-start(f32[3,2,64,384]{3,2,1,0:T(8,128)} %get-tuple-element.56), channel_id=1, source_target_pairs={{0,120},{8,0},{16,8},{24,16},{32,24},{40,32},{48,40},{56,48},{64,5... | collective-permute-start | bytes 1769480 | tf_op jit(solution)/shard_map/ppermute | solution.py:312
  27.1 0.7 fusion.3
  27.8 2.6 %collective-permute-start.2 = (f32[3,8,2,384]{3,2,1,0:T(2,128)}, f32[3,8,2,384]{3,2,1,0:T(2,128)S(1)}, u32[]{:S(2)}, u32[]{:S(2)}) collective-permute-start(f32[3,8,2,384]{3,2,1,0:T(2,128)} %get-tuple-element.55), channel_id=1, source_target_pairs={{0,1},{1,2},{2,3},{3,4},{4,5},{5,6},{6,7},{7,0},{8,9},{9,10},{10,1... | collective-permute-start | bytes 221192 | tf_op jit(solution)/shard_map/ppermute | solution.py:312
  30.5 2.9 %all-to-all-done = f32[64,16,128]{2,1,0:T(8,128)} async-done(((f32[64,16,128]{2,1,0:T(8,128)}), f32[64,16,128]{2,1,0:T(8,128)}, u32[]{:S(2)}, u32[]{:S(2)}) %all-to-all-start) | async-done | bytes 524320 | tf_op jit(solution)/shard_map/all_to_all | solution.py:324
  33.3 1.1 reduce_sum.67
  34.5 2.3 %collective-permute-start.4 = (f32[16,128]{1,0:T(8,128)S(1)}, f32[16,128]{1,0:T(8,128)S(1)}, u32[]{:S(2)}, u32[]{:S(2)}) collective-permute-start(f32[16,128]{1,0:T(8,128)S(1)} %reduce_sum.67), channel_id=1, source_target_pairs={{0,1},{1,0},{2,3},{3,2},{4,5},{5,4},{6,7},{7,6},{8,9},{9,8},{10,11... | collective-permute-start | bytes 24584 | tf_op jit(solution)/shard_map/ppermute | solution.py:326
  36.8 0.8 collective-permute-done.4
  37.6 7.7 %collective-permute-done.x_low = f32[3,2,64,384]{3,2,1,0:T(8,128)S(1)} collective-permute-done((f32[3,2,64,384]{3,2,1,0:T(8,128)}, f32[3,2,64,384]{3,2,1,0:T(8,128)S(1)}, u32[]{:S(2)}, u32[]{:S(2)}) %collective-permute-start) | collective-permute-done | bytes 589856 | tf_op jit(solution)/shard_map/ppermute | solution.py:312
  45.3 5.8 %one_step.4 = (f32[3,8,64,384]{3,2,1,0:T(8,128)S(1)}, f32[3,2,64,384]{3,2,1,0:T(8,128)S(1)}, f32[3,2,64,384]{3,2,1,0:T(8,128)S(1)}, f32[3,8,2,384]{3,2,1,0:T(2,1...) custom-call(s32[3,4]{1,0:T(4,128)S(1)} %bitcast.28, ...), custom_call_target="tpu_custom_call" | custom-call | tf_op jit(solution)/shard_map/one_step/pallas_call | solution.py:291
  51.1 1.4 copy-done.4
  52.5 0.8 copy-done.9
  53.3 0.8 copy-done.14
  54.1 0.8 copy-done.16
  54.9 0.6 copy-done.17
  55.6 0.6 copy-done.18
  56.2 5.7 %all-to-all-start.1 = ((f32[64,16,128]{2,1,0:T(8,128)}), f32[64,16,128]{2,1,0:T(8,128)S(1)}, u32[]{:S(2)}, u32[]{:S(2)}) async-start(f32[64,16,128]{2,1,0:T(8,128)} %copy-done.9), calls=%async_computation.1 | async-start | bytes 1048576 | tf_op jit(solution)/shard_map/all_to_all | solution.py:324
  61.9 1.1 collective-permute-start.5
  63.0 3.8 %collective-permute-start.6 = (f32[3,2,64,384]{3,2,1,0:T(8,128)}, f32[3,2,64,384]{3,2,1,0:T(8,128)S(1)}, u32[]{:S(2)}, u32[]{:S(2)}) collective-permute-start(f32[3,2,64,384]{3,2,1,0:T(8,128)} %copy-done.14), channel_id=1, source_target_pairs={{0,120},{8,0},{16,8},{24,16},{32,24},{40,32},{48,40},{56,48},{64,5... | collective-permute-start | bytes 1769480 | tf_op jit(solution)/shard_map/ppermute | solution.py:312
  66.8 7.5 %all-to-all-done.1 = f32[64,16,128]{2,1,0:T(8,128)S(1)} async-done(((f32[64,16,128]{2,1,0:T(8,128)}), f32[64,16,128]{2,1,0:T(8,128)S(1)}, u32[]{:S(2)}, u32[]{:S(2)}) %all-to-all-start.1) | async-done | bytes 524320 | tf_op jit(solution)/shard_map/all_to_all | solution.py:324
  74.4 2.1 %collective-permute-start.9 = (f32[16,128]{1,0:T(8,128)S(1)}, f32[16,128]{1,0:T(8,128)S(1)}, u32[]{:S(2)}, u32[]{:S(2)}) collective-permute-start(f32[16,128]{1,0:T(8,128)S(1)} %reduce_sum.68), channel_id=1, source_target_pairs={{0,1},{1,0},{2,3},{3,2},{4,5},{5,4},{6,7},{7,6},{8,9},{9,8},{10,11... | collective-permute-start | bytes 24584 | tf_op jit(solution)/shard_map/ppermute | solution.py:326
  77.3 1.0 collective-permute-done.7.y_low
  78.4 2.6 %collective-permute-done.8.y_high = f32[3,8,2,384]{3,2,1,0:T(2,128)S(1)} collective-permute-done((f32[3,8,2,384]{3,2,1,0:T(2,128)}, f32[3,8,2,384]{3,2,1,0:T(2,128)S(1)}, u32[]{:S(2)}, u32[]{:S(2)}) %collective-permute-start.8) | collective-permute-done | bytes 73760 | tf_op jit(solution)/shard_map/ppermute | solution.py:312
  81.0 4.1 %collective-permute-done.5.x_low = f32[3,2,64,384]{3,2,1,0:T(8,128)S(1)} collective-permute-done((f32[3,2,64,384]{3,2,1,0:T(8,128)}, f32[3,2,64,384]{3,2,1,0:T(8,128)S(1)}, u32[]{:S(2)}, u32[]{:S(2)}) %collective-permute-start.5) | collective-permute-done | bytes 589856 | tf_op jit(solution)/shard_map/ppermute | solution.py:312
  85.1 1.7 copy-done.5
  86.7 5.7 %one_step.5 = (f32[3,8,64,384]{3,2,1,0:T(8,128)S(1)}, f32[3,2,64,384]{3,2,1,0:T(8,128)S(1)}, f32[3,2,64,384]{3,2,1,0:T(8,128)S(1)}, f32[3,8,2,384]{3,2,1,0:T(2,1...) custom-call(s32[3,4]{1,0:T(4,128)S(1)} %bitcast.29, s32[1,4]{1,0:T(1,128)S(1)} %copy-done.12, ...), custom_call_target="tpu_custom_call" | custom-call | tf_op jit(solution)/shard_map/one_step/pallas_call | solution.py:291
  92.5 1.4 copy-done.2
  93.9 6.7 %all-to-all-start.2 = ((f32[64,16,128]{2,1,0:T(8,128)}), f32[64,16,128]{2,1,0:T(8,128)S(1)}, u32[]{:S(2)}, u32[]{:S(2)}) async-start(f32[64,16,128]{2,1,0:T(8,128)} %get-tuple-element.43), calls=%async_computation.2 | async-start | bytes 1048576 | tf_op jit(solution)/shard_map/all_to_all | solution.py:324
  100.6 1.1 collective-permute-start.10
  101.6 3.8 %collective-permute-start.11 = (f32[3,2,64,384]{3,2,1,0:T(8,128)S(1)}, f32[3,2,64,384]{3,2,1,0:T(8,128)S(1)}, u32[]{:S(2)}, u32[]{:S(2)}) collective-permute-start(f32[3,2,64,384]{3,2,1,0:T(8,128)S(1)} %get-tuple-element.40), channel_id=1, source_target_pairs={{0,120},{8,0},{16,8},{24,16},{32,24},{40,32},{48,40},{56,48},{64,5... | collective-permute-start | bytes 1769480 | tf_op jit(solution)/shard_map/ppermute | solution.py:312
  105.4 7.5 %all-to-all-done.2 = f32[64,16,128]{2,1,0:T(8,128)S(1)} async-done(((f32[64,16,128]{2,1,0:T(8,128)}), f32[64,16,128]{2,1,0:T(8,128)S(1)}, u32[]{:S(2)}, u32[]{:S(2)}) %all-to-all-start.2) | async-done | bytes 524320 | tf_op jit(solution)/shard_map/all_to_all | solution.py:324
  113.0 2.2 %collective-permute-start.14 = (f32[16,128]{1,0:T(8,128)S(1)}, f32[16,128]{1,0:T(8,128)S(1)}, u32[]{:S(2)}, u32[]{:S(2)}) collective-permute-start(f32[16,128]{1,0:T(8,128)S(1)} %reduce_sum.69), channel_id=1, source_target_pairs={{0,1},{1,0},{2,3},{3,2},{4,5},{5,4},{6,7},{7,6},{8,9},{9,8},{10,11... | collective-permute-start | bytes 24584 | tf_op jit(solution)/shard_map/ppermute | solution.py:326
  116.0 0.7 collective-permute-done.12.y_low
  116.7 2.7 %collective-permute-done.13.y_high = f32[3,8,2,384]{3,2,1,0:T(2,128)S(1)} collective-permute-done((f32[3,8,2,384]{3,2,1,0:T(2,128)S(1)}, f32[3,8,2,384]{3,2,1,0:T(2,128)S(1)}, u32[]{:S(2)}, u32[]{:S(2)}) %collective-permute-start.13) | collective-permute-done | bytes 73760 | tf_op jit(solution)/shard_map/ppermute | solution.py:312
  119.4 4.3 %collective-permute-done.10.x_low = f32[3,2,64,384]{3,2,1,0:T(8,128)S(1)} collective-permute-done((f32[3,2,64,384]{3,2,1,0:T(8,128)S(1)}, f32[3,2,64,384]{3,2,1,0:T(8,128)S(1)}, u32[]{:S(2)}, u32[]{:S(2)}) %collective-permute-start.10) | collective-permute-done | bytes 589856 | tf_op jit(solution)/shard_map/ppermute | solution.py:312
  123.7 0.8 copy-done.6
  124.5 1.7 copy-done.3
  126.2 1.1 copy-done.7
  127.3 4.9 %one_step.6 = (f32[3,8,64,384]{3,2,1,0:T(8,128)S(1)}, f32[3,2,64,384]{3,2,1,0:T(8,128)S(1)}, f32[3,2,64,384]{3,2,1,0:T(8,128)S(1)}, f32[3,8,2,384]{3,2,1,0:T(2,1...) custom-call(s32[3,4]{1,0:T(4,128)S(1)} %bitcast.30, ...), custom_call_target="tpu_custom_call" | custom-call | tf_op jit(solution)/shard_map/one_step/pallas_call | solution.py:291
  132.2 0.8 copy-done.8
  133.0 0.8 copy-done.13
  133.8 0.8 copy-done.15
  134.6 7.0 %all-to-all-start.3 = ((f32[64,16,128]{2,1,0:T(8,128)}), f32[64,16,128]{2,1,0:T(8,128)}, u32[]{:S(2)}, u32[]{:S(2)}) async-start(f32[64,16,128]{2,1,0:T(8,128)} %copy-done.8), calls=%async_computation.3 | async-start | bytes 1048576 | tf_op jit(solution)/shard_map/all_to_all | solution.py:324
  141.6 1.0 collective-permute-start.15
  142.6 3.8 %collective-permute-start.16 = (f32[3,2,64,384]{3,2,1,0:T(8,128)}, f32[3,2,64,384]{3,2,1,0:T(8,128)}, u32[]{:S(2)}, u32[]{:S(2)}) collective-permute-start(f32[3,2,64,384]{3,2,1,0:T(8,128)} %copy-done.13), channel_id=1, source_target_pairs={{0,120},{8,0},{16,8},{24,16},{32,24},{40,32},{48,40},{56,48},{64,5... | collective-permute-start | bytes 1769480 | tf_op jit(solution)/shard_map/ppermute | solution.py:312
  146.5 7.4 %all-to-all-done.3 = f32[64,16,128]{2,1,0:T(8,128)} async-done(((f32[64,16,128]{2,1,0:T(8,128)}), f32[64,16,128]{2,1,0:T(8,128)}, u32[]{:S(2)}, u32[]{:S(2)}) %all-to-all-start.3) | async-done | bytes 524320 | tf_op jit(solution)/shard_map/all_to_all | solution.py:324
  153.8 1.1 reduce_sum.70
  154.9 2.2 %collective-permute-start.19 = (f32[16,128]{1,0:T(8,128)S(1)}, f32[16,128]{1,0:T(8,128)S(1)}, u32[]{:S(2)}, u32[]{:S(2)}) collective-permute-start(f32[16,128]{1,0:T(8,128)S(1)} %reduce_sum.70), channel_id=1, source_target_pairs={{0,1},{1,0},{2,3},{3,2},{4,5},{5,4},{6,7},{7,6},{8,9},{9,8},{10,11... | collective-permute-start | bytes 24584 | tf_op jit(solution)/shard_map/ppermute | solution.py:326
  157.9 0.8 collective-permute-done.17.y_low
  158.8 2.8 %collective-permute-done.18.y_high = f32[3,8,2,384]{3,2,1,0:T(2,128)S(1)} collective-permute-done((f32[3,8,2,384]{3,2,1,0:T(2,128)S(1)}, f32[3,8,2,384]{3,2,1,0:T(2,128)S(1)}, u32[]{:S(2)}, u32[]{:S(2)}) %collective-permute-start.18) | collective-permute-done | bytes 73760 | tf_op jit(solution)/shard_map/ppermute | solution.py:312
  161.5 3.3 %collective-permute-done.15.x_low = f32[3,2,64,384]{3,2,1,0:T(8,128)S(1)} collective-permute-done((f32[3,2,64,384]{3,2,1,0:T(8,128)}, f32[3,2,64,384]{3,2,1,0:T(8,128)S(1)}, u32[]{:S(2)}, u32[]{:S(2)}) %collective-permute-start.15) | collective-permute-done | bytes 589856 | tf_op jit(solution)/shard_map/ppermute | solution.py:312
  164.8 6.6 %one_step.7 = (f32[3,8,64,384]{3,2,1,0:T(8,128)}, f32[16,128]{1,0:T(8,128)S(1)}) custom-call(s32[3,4]{1,0:T(4,128)S(1)} %bitcast.31, s32[1,4]{1,0:T(1,128)S(1)} %copy-done.12, f32[3,8,64,384]{3,2,1,0:T(8,128)S(1)} %get-tuple-element.45.velocity, f32[3,2,64,384]{3,2,1,0:T(8,128)S(1)} %collective-permute-done.15.x_low, ...), custom_call_target="tpu_custom_call" | custom-call | tf_op jit(solution)/shard_map/one_step/pallas_call | solution.py:291
  171.4 0.5 slice_bitcast_fusion
  172.0 0.6 div.10
  (59 shorter events, 3.4 us)
Async XLA Ops:
  3.7 1.7 copy-start
  5.3 0.8 copy-start.10
  6.1 0.7 copy-start.11
  6.7 14.5 %copy-start.1 = (f32[3,8,64,384]{3,2,1,0:T(8,128)S(1)}, f32[3,8,64,384]{3,2,1,0:T(8,128)}, u32[]{:S(2)}) copy-start(f32[3,8,64,384]{3,2,1,0:T(8,128)} %velocity.3) | copy-start | bytes 7077892
  8.8 21.6 %copy-start.21 = (s32[100]{0:T(128)S(1)}, s32[100]{0:T(128)}, u32[]{:S(2)}) copy-start(s32[100]{0:T(128)} %param.14) | copy-start | bytes 1204
  8.9 27.9 %copy-start.19 = (f32[2,384]{1,0:T(2,128)S(1)}, f32[2,384]{1,0:T(2,128)}, u32[]{:S(2)}) copy-start(f32[2,384]{1,0:T(2,128)} %param.9) | copy-start | bytes 9220
  8.9 36.4 %copy-start.12 = (s32[1,4]{1,0:T(1,128)S(1)}, s32[1,4]{1,0:T(1,128)}, u32[]{:S(2)}) copy-start(s32[1,4]{1,0:T(1,128)} %ids.9) | copy-start | bytes 52
  8.9 24.5 %all-to-all-start = ((f32[64,16,128]{2,1,0:T(8,128)}), f32[64,16,128]{2,1,0:T(8,128)}, u32[]{:S(2)}, u32[]{:S(2)}) async-start(f32[64,16,128]{2,1,0:T(8,128)} %get-tuple-element.29), calls=%async_computation | async-start | bytes 1048576 | tf_op jit(solution)/shard_map/all_to_all | solution.py:324
  22.3 22.9 %collective-permute-start = (f32[3,2,64,384]{3,2,1,0:T(8,128)}, f32[3,2,64,384]{3,2,1,0:T(8,128)S(1)}, u32[]{:S(2)}, u32[]{:S(2)}) collective-permute-start(f32[3,2,64,384]{3,2,1,0:T(8,128)} %get-tuple-element.57), channel_id=1, source_target_pairs={{0,8},{8,16},{16,24},{24,32},{32,40},{40,48},{48,56},{56,64},{64,7... | collective-permute-start | bytes 1769480 | tf_op jit(solution)/shard_map/ppermute | solution.py:312
  23.3 22.0 %collective-permute-start.1 = (f32[3,2,64,384]{3,2,1,0:T(8,128)}, f32[3,2,64,384]{3,2,1,0:T(8,128)}, u32[]{:S(2)}, u32[]{:S(2)}) collective-permute-start(f32[3,2,64,384]{3,2,1,0:T(8,128)} %get-tuple-element.56), channel_id=1, source_target_pairs={{0,120},{8,0},{16,8},{24,16},{32,24},{40,32},{48,40},{56,48},{64,5... | collective-permute-start | bytes 1769480 | tf_op jit(solution)/shard_map/ppermute | solution.py:312
  27.8 9.7 %collective-permute-start.2 = (f32[3,8,2,384]{3,2,1,0:T(2,128)}, f32[3,8,2,384]{3,2,1,0:T(2,128)S(1)}, u32[]{:S(2)}, u32[]{:S(2)}) collective-permute-start(f32[3,8,2,384]{3,2,1,0:T(2,128)} %get-tuple-element.55), channel_id=1, source_target_pairs={{0,1},{1,2},{2,3},{3,4},{4,5},{5,6},{6,7},{7,0},{8,9},{9,10},{10,1... | collective-permute-start | bytes 221192 | tf_op jit(solution)/shard_map/ppermute | solution.py:312
  30.5 7.1 %collective-permute-start.3 = (f32[3,8,2,384]{3,2,1,0:T(2,128)}, f32[3,8,2,384]{3,2,1,0:T(2,128)S(1)}, u32[]{:S(2)}, u32[]{:S(2)}) collective-permute-start(f32[3,8,2,384]{3,2,1,0:T(2,128)} %get-tuple-element.54), channel_id=1, source_target_pairs={{0,7},{1,0},{2,1},{3,2},{4,3},{5,4},{6,5},{7,6},{8,15},{9,8},{10,9... | collective-permute-start | bytes 221192 | tf_op jit(solution)/shard_map/ppermute | solution.py:312
  34.5 3.1 %collective-permute-start.4 = (f32[16,128]{1,0:T(8,128)S(1)}, f32[16,128]{1,0:T(8,128)S(1)}, u32[]{:S(2)}, u32[]{:S(2)}) collective-permute-start(f32[16,128]{1,0:T(8,128)S(1)} %reduce_sum.67), channel_id=1, source_target_pairs={{0,1},{1,0},{2,3},{3,2},{4,5},{5,4},{6,7},{7,6},{8,9},{9,8},{10,11... | collective-permute-start | bytes 24584 | tf_op jit(solution)/shard_map/ppermute | solution.py:326
  51.1 1.4 copy-start.4
  52.5 0.8 copy-start.9
  53.3 0.8 copy-start.14
  54.1 0.8 copy-start.16
  54.9 0.6 copy-start.17
  55.6 0.6 copy-start.18
  56.2 18.1 %all-to-all-start.1 = ((f32[64,16,128]{2,1,0:T(8,128)}), f32[64,16,128]{2,1,0:T(8,128)S(1)}, u32[]{:S(2)}, u32[]{:S(2)}) async-start(f32[64,16,128]{2,1,0:T(8,128)} %copy-done.9), calls=%async_computation.1 | async-start | bytes 1048576 | tf_op jit(solution)/shard_map/all_to_all | solution.py:324
  61.9 23.2 %collective-permute-start.5 = (f32[3,2,64,384]{3,2,1,0:T(8,128)}, f32[3,2,64,384]{3,2,1,0:T(8,128)S(1)}, u32[]{:S(2)}, u32[]{:S(2)}) collective-permute-start(f32[3,2,64,384]{3,2,1,0:T(8,128)} %copy-done.16), channel_id=1, source_target_pairs={{0,8},{8,16},{16,24},{24,32},{32,40},{40,48},{48,56},{56,64},{64,7... | collective-permute-start | bytes 1769480 | tf_op jit(solution)/shard_map/ppermute | solution.py:312
  63.0 22.1 %collective-permute-start.6 = (f32[3,2,64,384]{3,2,1,0:T(8,128)}, f32[3,2,64,384]{3,2,1,0:T(8,128)S(1)}, u32[]{:S(2)}, u32[]{:S(2)}) collective-permute-start(f32[3,2,64,384]{3,2,1,0:T(8,128)} %copy-done.14), channel_id=1, source_target_pairs={{0,120},{8,0},{16,8},{24,16},{32,24},{40,32},{48,40},{56,48},{64,5... | collective-permute-start | bytes 1769480 | tf_op jit(solution)/shard_map/ppermute | solution.py:312
  74.4 3.0 %collective-permute-start.9 = (f32[16,128]{1,0:T(8,128)S(1)}, f32[16,128]{1,0:T(8,128)S(1)}, u32[]{:S(2)}, u32[]{:S(2)}) collective-permute-start(f32[16,128]{1,0:T(8,128)S(1)} %reduce_sum.68), channel_id=1, source_target_pairs={{0,1},{1,0},{2,3},{3,2},{4,5},{5,4},{6,7},{7,6},{8,9},{9,8},{10,11... | collective-permute-start | bytes 24584 | tf_op jit(solution)/shard_map/ppermute | solution.py:326
  76.5 1.9 %collective-permute-start.7 = (f32[3,8,2,384]{3,2,1,0:T(2,128)}, f32[3,8,2,384]{3,2,1,0:T(2,128)S(1)}, u32[]{:S(2)}, u32[]{:S(2)}) collective-permute-start(f32[3,8,2,384]{3,2,1,0:T(2,128)} %copy-done.18), channel_id=1, source_target_pairs={{0,1},{1,2},{2,3},{3,4},{4,5},{5,6},{6,7},{7,0},{8,9},{9,10},{10,1... | collective-permute-start | bytes 221192 | tf_op jit(solution)/shard_map/ppermute | solution.py:312
  76.7 4.3 %collective-permute-start.8 = (f32[3,8,2,384]{3,2,1,0:T(2,128)}, f32[3,8,2,384]{3,2,1,0:T(2,128)S(1)}, u32[]{:S(2)}, u32[]{:S(2)}) collective-permute-start(f32[3,8,2,384]{3,2,1,0:T(2,128)} %copy-done.17), channel_id=1, source_target_pairs={{0,7},{1,0},{2,1},{3,2},{4,3},{5,4},{6,5},{7,6},{8,15},{9,8},{10,9... | collective-permute-start | bytes 221192 | tf_op jit(solution)/shard_map/ppermute | solution.py:312
  85.1 1.7 copy-start.5
  92.5 1.4 copy-start.2
  93.9 19.1 %all-to-all-start.2 = ((f32[64,16,128]{2,1,0:T(8,128)}), f32[64,16,128]{2,1,0:T(8,128)S(1)}, u32[]{:S(2)}, u32[]{:S(2)}) async-start(f32[64,16,128]{2,1,0:T(8,128)} %get-tuple-element.43), calls=%async_computation.2 | async-start | bytes 1048576 | tf_op jit(solution)/shard_map/all_to_all | solution.py:324
  100.6 23.1 %collective-permute-start.10 = (f32[3,2,64,384]{3,2,1,0:T(8,128)S(1)}, f32[3,2,64,384]{3,2,1,0:T(8,128)S(1)}, u32[]{:S(2)}, u32[]{:S(2)}) collective-permute-start(f32[3,2,64,384]{3,2,1,0:T(8,128)S(1)} %get-tuple-element.39), channel_id=1, source_target_pairs={{0,8},{8,16},{16,24},{24,32},{32,40},{40,48},{48,56},{56,64},{64,7... | collective-permute-start | bytes 1769480 | tf_op jit(solution)/shard_map/ppermute | solution.py:312
  101.6 22.1 %collective-permute-start.11 = (f32[3,2,64,384]{3,2,1,0:T(8,128)S(1)}, f32[3,2,64,384]{3,2,1,0:T(8,128)S(1)}, u32[]{:S(2)}, u32[]{:S(2)}) collective-permute-start(f32[3,2,64,384]{3,2,1,0:T(8,128)S(1)} %get-tuple-element.40), channel_id=1, source_target_pairs={{0,120},{8,0},{16,8},{24,16},{32,24},{40,32},{48,40},{56,48},{64,5... | collective-permute-start | bytes 1769480 | tf_op jit(solution)/shard_map/ppermute | solution.py:312
  113.0 3.0 %collective-permute-start.14 = (f32[16,128]{1,0:T(8,128)S(1)}, f32[16,128]{1,0:T(8,128)S(1)}, u32[]{:S(2)}, u32[]{:S(2)}) collective-permute-start(f32[16,128]{1,0:T(8,128)S(1)} %reduce_sum.69), channel_id=1, source_target_pairs={{0,1},{1,0},{2,3},{3,2},{4,5},{5,4},{6,7},{7,6},{8,9},{9,8},{10,11... | collective-permute-start | bytes 24584 | tf_op jit(solution)/shard_map/ppermute | solution.py:326
  115.2 1.6 collective-permute-start.12
  115.3 4.1 %collective-permute-start.13 = (f32[3,8,2,384]{3,2,1,0:T(2,128)S(1)}, f32[3,8,2,384]{3,2,1,0:T(2,128)S(1)}, u32[]{:S(2)}, u32[]{:S(2)}) collective-permute-start(f32[3,8,2,384]{3,2,1,0:T(2,128)S(1)} %get-tuple-element.42), channel_id=1, source_target_pairs={{0,7},{1,0},{2,1},{3,2},{4,3},{5,4},{6,5},{7,6},{8,15},{9,8},{10,9... | collective-permute-start | bytes 221192 | tf_op jit(solution)/shard_map/ppermute | solution.py:312
  123.7 0.8 copy-start.6
  124.5 1.7 copy-start.3
  126.2 1.1 copy-start.7
  132.2 0.8 copy-start.8
  133.0 0.8 copy-start.13
  133.8 0.8 copy-start.15
  134.6 19.2 %all-to-all-start.3 = ((f32[64,16,128]{2,1,0:T(8,128)}), f32[64,16,128]{2,1,0:T(8,128)}, u32[]{:S(2)}, u32[]{:S(2)}) async-start(f32[64,16,128]{2,1,0:T(8,128)} %copy-done.8), calls=%async_computation.3 | async-start | bytes 1048576 | tf_op jit(solution)/shard_map/all_to_all | solution.py:324
  141.6 23.2 %collective-permute-start.15 = (f32[3,2,64,384]{3,2,1,0:T(8,128)}, f32[3,2,64,384]{3,2,1,0:T(8,128)S(1)}, u32[]{:S(2)}, u32[]{:S(2)}) collective-permute-start(f32[3,2,64,384]{3,2,1,0:T(8,128)} %copy-done.15), channel_id=1, source_target_pairs={{0,8},{8,16},{16,24},{24,32},{32,40},{40,48},{48,56},{56,64},{64,7... | collective-permute-start | bytes 1769480 | tf_op jit(solution)/shard_map/ppermute | solution.py:312
  142.6 30.0 %copy-start.20 = (f32[1,4]{1,0:T(1,128)S(1)}, f32[1,4]{1,0:T(1,128)}, u32[]{:S(2)}) copy-start(f32[1,4]{1,0:T(1,128)} %param.15) | copy-start | bytes 52
  142.6 22.2 %collective-permute-start.16 = (f32[3,2,64,384]{3,2,1,0:T(8,128)}, f32[3,2,64,384]{3,2,1,0:T(8,128)}, u32[]{:S(2)}, u32[]{:S(2)}) collective-permute-start(f32[3,2,64,384]{3,2,1,0:T(8,128)} %copy-done.13), channel_id=1, source_target_pairs={{0,120},{8,0},{16,8},{24,16},{32,24},{40,32},{48,40},{56,48},{64,5... | collective-permute-start | bytes 1769480 | tf_op jit(solution)/shard_map/ppermute | solution.py:312
  154.9 3.0 %collective-permute-start.19 = (f32[16,128]{1,0:T(8,128)S(1)}, f32[16,128]{1,0:T(8,128)S(1)}, u32[]{:S(2)}, u32[]{:S(2)}) collective-permute-start(f32[16,128]{1,0:T(8,128)S(1)} %reduce_sum.70), channel_id=1, source_target_pairs={{0,1},{1,0},{2,3},{3,2},{4,5},{5,4},{6,7},{7,6},{8,9},{9,8},{10,11... | collective-permute-start | bytes 24584 | tf_op jit(solution)/shard_map/ppermute | solution.py:326
  157.2 1.6 collective-permute-start.17
  157.3 4.2 %collective-permute-start.18 = (f32[3,8,2,384]{3,2,1,0:T(2,128)S(1)}, f32[3,8,2,384]{3,2,1,0:T(2,128)S(1)}, u32[]{:S(2)}, u32[]{:S(2)}) collective-permute-start(f32[3,8,2,384]{3,2,1,0:T(2,128)S(1)} %get-tuple-element.49), channel_id=1, source_target_pairs={{0,7},{1,0},{2,1},{3,2},{4,3},{5,4},{6,5},{7,6},{8,15},{9,8},{10,9... | collective-permute-start | bytes 221192 | tf_op jit(solution)/shard_map/ppermute | solution.py:312
